TPU v7x, 8 devices: a whole 2x2x1 slice. The times are simulated.
8 devices in a mesh: data: 2 (over z, y), dap: 4 (over x, core).
Axes of the slice: x: 2, y: 2, z: 1, core: 2. Of those that a mesh axis runs over, the one named last changes fastest.
Arguments:
- msa_act: bfloat16 [4, 128, 128, 256], P('data', 'dap'), parts along dimension 0
- pair_act: bfloat16 [4, 128, 128, 128], P('data', 'dap'), parts along dimension 0
- msa_mask: int32 [4, 128, 128], P('data'), parts along dimension 0
- res_mask: int32 [4, 128], P('data'), parts along dimension 0
- w_row_bias: bfloat16 [128, 8], replicated
- w_row_qkvg: bfloat16 [256, 4, 8, 32], replicated
- w_row_out: bfloat16 [8, 32, 256], replicated
- w_col_qkvg: bfloat16 [256, 4, 8, 32], replicated
- w_col_out: bfloat16 [8, 32, 256], replicated
- w_opm_ac: bfloat16 [256, 2, 32], replicated
- w_opm_out: bfloat16 [32, 32, 128], replicated
- w_ts_bias: bfloat16 [128, 4], replicated
- w_ts_qkvg: bfloat16 [128, 4, 4, 32], replicated
- w_ts_out: bfloat16 [4, 32, 128], replicated
- w_te_bias: bfloat16 [128, 4], replicated
- w_te_qkvg: bfloat16 [128, 4, 4, 32], replicated
- w_te_out: bfloat16 [4, 32, 128], replicated
Outputs:
- output 1: bfloat16 [4, 128, 128, 256], P('data', 'dap'), parts along dimension 0
- output 2: bfloat16 [4, 128, 128, 128], P('data', 'dap'), parts along dimension 0
There are 2 independent parts. A program takes and returns all parts, laid end to end along the dimension named above; an argument that names none is the same for every part.
All inputs are finite; a program needn't handle non-finite values.
Results may differ from a plain program's by a relative error of at most 0.0153101.
Values are sent between devices in bfloat16 or wider.
A program may use at most 1 GiB of HBM per device.

v0:
```python
import jax
import jax.numpy as jnp
from jax import lax
from jax.sharding import PartitionSpec as P

SCORE_ELEMS = 8388608
MASK_SCALE = 10000.0
LN_EPS = 1e-5
OPM_EPS = 1e-3
N_WEIGHTS = 13
PART_AXIS = 'data'
GROUP_AXIS = 'dap'


def layer_norm(tensor):
    x_float = tensor.astype(jnp.float32)
    mean_val = jnp.mean(x_float, axis=-1, keepdims=True)
    centred = x_float - mean_val
    var_val = jnp.mean(centred * centred, axis=-1, keepdims=True)
    return (centred * lax.rsqrt(var_val + LN_EPS)).astype(jnp.bfloat16)


def mask_to_bias(mask):
    return (mask.astype(jnp.float32) - 1.0) * MASK_SCALE


def rows_per_map(n_rows, per_row):
    return max(1, min(n_rows, SCORE_ELEMS // per_row))


def gated_attention(x_row, normed, key_bias, pair_bias, w_qkvg, w_out):
    proj_all = jnp.einsum('lc,cghd->glhd', normed, w_qkvg, preferred_element_type=jnp.float32)
    queries = proj_all[0].astype(jnp.bfloat16)
    keys_bf = proj_all[1].astype(jnp.bfloat16)
    values_bf = proj_all[2].astype(jnp.bfloat16)
    gate_sig = jax.nn.sigmoid(proj_all[3])
    inv_sqrt = queries.shape[-1] ** -0.5
    logits = jnp.einsum('qhd,khd->hqk', queries, keys_bf, preferred_element_type=jnp.float32) * inv_sqrt + key_bias
    if pair_bias is not None:
        logits = logits + pair_bias
    attn_prob = jax.nn.softmax(logits, axis=-1).astype(jnp.bfloat16)
    mixed = jnp.einsum('hqk,khd->qhd', attn_prob, values_bf, preferred_element_type=jnp.float32) * gate_sig
    update = jnp.einsum('qhd,hdc->qc', mixed.astype(jnp.bfloat16), w_out, preferred_element_type=jnp.float32)
    return (x_row.astype(jnp.float32) + update).astype(jnp.bfloat16)


def attend_rows(row_stack, normed, key_rows, pair_bias, w_qkvg, w_out):
    n_rows = row_stack.shape[0]
    length = row_stack.shape[1]
    n_heads = w_qkvg.shape[2]
    return lax.map(lambda row_in: gated_attention(row_in[0], row_in[1], row_in[2], pair_bias, w_qkvg, w_out),
                   (row_stack, normed, key_rows), batch_size=rows_per_map(n_rows, n_heads * length * length))


def gathered_bias(normed, w_bias):
    bias_part = jnp.einsum('ijc,ch->hij', normed, w_bias, preferred_element_type=jnp.float32).astype(jnp.bfloat16)
    return lax.all_gather(bias_part, GROUP_AXIS, axis=1, tiled=True)


def triangle_rows(pair_rows, res_mask, w_bias, w_qkvg, w_out):
    normed = layer_norm(pair_rows)
    key_rows = jnp.broadcast_to(mask_to_bias(res_mask)[None, :], (pair_rows.shape[0], res_mask.shape[0]))
    return attend_rows(pair_rows, normed, key_rows, gathered_bias(normed, w_bias), w_qkvg, w_out)


def outer_rows(pair_rows, left_proj, right_proj, norm_pairs, w_opm_out):
    n_rows = pair_rows.shape[0]
    n_res = right_proj.shape[0]
    width = right_proj.shape[2]

    def one_row(row_in):
        left_row, norm_row, pair_row = row_in
        outer = jnp.einsum('se,jsf->jef', left_row, right_proj, preferred_element_type=jnp.float32)
        outer = outer / (norm_row[:, None, None] + OPM_EPS)
        update = jnp.einsum('jef,efc->jc', outer.astype(jnp.bfloat16), w_opm_out, preferred_element_type=jnp.float32)
        return (pair_row.astype(jnp.float32) + update).astype(jnp.bfloat16)

    return lax.map(one_row, (left_proj, norm_pairs, pair_rows), batch_size=rows_per_map(n_rows, n_res * width * width))


def crop_block(piece_d8, pair_rows, local_c8, res_mask, weights):
    (w_row_bias, w_row_qkvg, w_row_out, w_col_qkvg, w_col_out, w_opm_ac, w_opm_out,
     w_ts_bias, w_ts_qkvg, w_ts_out, w_te_bias, w_te_qkvg, w_te_out) = weights
    dev_index = lax.axis_index(GROUP_AXIS)
    seq_local = piece_d8.shape[0]
    res_local = pair_rows.shape[0]
    row_bias = gathered_bias(layer_norm(pair_rows), w_row_bias)
    seq_mask = lax.dynamic_slice_in_dim(local_c8, dev_index * seq_local, seq_local, axis=0)
    piece_d8 = attend_rows(piece_d8, layer_norm(piece_d8), mask_to_bias(seq_mask), row_bias, w_row_qkvg, w_row_out)
    value_a8 = jnp.swapaxes(lax.all_to_all(piece_d8, GROUP_AXIS, 1, 0, tiled=True), 0, 1)
    col_mask = jnp.swapaxes(lax.dynamic_slice_in_dim(local_c8, dev_index * res_local, res_local, axis=1), 0, 1)
    value_a8 = attend_rows(value_a8, layer_norm(value_a8), mask_to_bias(col_mask), None, w_col_qkvg, w_col_out)
    col_mask_bf = col_mask.astype(jnp.bfloat16)
    proj_ac = jnp.einsum('isc,cpe->pise', layer_norm(value_a8), w_opm_ac,
                         preferred_element_type=jnp.float32).astype(jnp.bfloat16)
    left_proj = proj_ac[0] * col_mask_bf[:, :, None]
    right_proj = lax.all_gather(proj_ac[1] * col_mask_bf[:, :, None], GROUP_AXIS, axis=0, tiled=True)
    norm_pairs = jnp.dot(col_mask_bf, local_c8.astype(jnp.bfloat16), preferred_element_type=jnp.float32)
    pair_rows = outer_rows(pair_rows, left_proj, right_proj, norm_pairs, w_opm_out)
    pair_rows = triangle_rows(pair_rows, res_mask, w_ts_bias, w_ts_qkvg, w_ts_out)
    pair_cols = jnp.swapaxes(lax.all_to_all(pair_rows, GROUP_AXIS, 1, 0, tiled=True), 0, 1)
    pair_cols = triangle_rows(pair_cols, res_mask, w_te_bias, w_te_qkvg, w_te_out)
    pair_out = lax.all_to_all(jnp.swapaxes(pair_cols, 0, 1), GROUP_AXIS, 0, 1, tiled=True)
    local_c7 = jnp.swapaxes(lax.all_to_all(value_a8, GROUP_AXIS, 1, 0, tiled=True), 0, 1)
    return local_c7, pair_out


def solution(mesh):
    rows_spec = P(PART_AXIS, GROUP_AXIS, None, None)
    in_specs = (rows_spec, rows_spec, P(PART_AXIS, None, None), P(PART_AXIS, None)) + (P(),) * N_WEIGHTS

    def local_block(value_a7, pair_act, local_c8, res_mask, *weights):
        array_b8 = []
        pair_list = []
        for crop_idx in range(value_a7.shape[0]):
            array_b7, pair_new = crop_block(value_a7[crop_idx], pair_act[crop_idx], local_c8[crop_idx],
                                           res_mask[crop_idx], weights)
            array_b8.append(array_b7)
            pair_list.append(pair_new)
        return jnp.stack(array_b8), jnp.stack(pair_list)

    return jax.shard_map(local_block, mesh=mesh, in_specs=in_specs, out_specs=(rows_spec, rows_spec),
                         check_vma=False)
```

profile of v0, /device:TPU:0, one launch (start us, length us, event | category | flops | bytes accessed | tf_op | source)
XLA Modules:
  0.0 665.2 jit_solution(4796441927437485974)
XLA Ops:
  12.5 10.8 %all_gather.24 = bf16[8,128,128]{2,0,1:T(8,128)(2,1)S(1)} all-gather(bf16[8,32,128]{2,0,1:T(8,128)(2,1)S(1)} %fusion.192), channel_id=1, replica_groups=mesh['data'=2,'dap'=4] {'dap'}, dimensions={1}, use_global_device_ids=true | all-gather | bytes 327680 | tf_op jit(solution)/shard_map/all_gather | solution.py:57
  29.8 10.9 %fusion.292 = (bf16[32,4,128,8,32]{2,4,3,1,0:T(8,128)(2,1)}, f32[32,4,128,8,32]{2,4,3,1,0:T(8,128)}) fusion(bf16[256,4,8,32]{0,3,2,1:T(8,128)(2,1)S(1)} %copy-done, f32[32,128]{1,0:T(8,128)S(1)} %add_rsqrt_fusion.11, f32[32,128]{1,0:T(8,128)S(1)} %get-tuple-element.257, bf16[2,32,128,256]{3,2,1,0:T(8,128)(2,1)} %param.17), kind=kOutput, calls=%fused_computation.420 | convolution fusion | flops 2155872256 | bytes 27820032 | tf_op jit(solution)/shard_map/while/body/eval_jaxpr/vmap(lc,cghd->glhd)/dot_general | solution.py:32
  40.7 12.4 %fusion.293 = (f32[32,8,128]{2,1,0:T(8,128)S(1)}, f32[32,8,128,128]{2,3,1,0:T(8,128)}) fusion(f32[8,128,128]{1,2,0:T(8,128)S(1)} %copy.135, f32[32,128]{1,0:T(8,128)S(1)} %multiply_bitcast_fusion.3, bf16[32,4,128,8,32]{2,4,3,1,0:T(8,128)(2,1)} %get-tuple-element.188), kind=kOutput, calls=%fused_computation.421 | convolution fusion | flops 289407104 | bytes 21643264 | tf_op jit(solution)/shard_map/while/body/eval_jaxpr/vmap()/sub | solution.py:41
  53.1 11.0 %fusion.56 = bf16[32,128,256]{2,1,0:T(8,128)(2,1)} fusion(bf16[2,32,128,256]{3,2,1,0:T(8,128)(2,1)} %param.17, f32[32,4,128,8,32]{2,4,3,1,0:T(8,128)} %get-tuple-element.189, f32[32,8,128,128]{2,3,1,0:T(8,128)} %get-tuple-element.198, f32[32,8,128]{2,1,0:T(8,128)S(1)} %get-tuple-element.190, bf16[32,4,128,8,32]{2,4,3,1,0:T(8,128)(2,1)} %get-tuple-element.188, ...), kind=kOutput, calls=%fused_computation.92 | convolution fusion | flops 822083584 | bytes 27525120 | tf_op jit(solution)/shard_map/while/body/eval_jaxpr/vmap(qhd,hdc->qc)/dot_general | solution.py:43
  74.5 27.1 %all_gather.25 = bf16[8,128,128]{2,0,1:T(8,128)(2,1)S(1)} all-gather(bf16[8,32,128]{2,0,1:T(8,128)(2,1)S(1)} %fusion.193), channel_id=1, replica_groups=mesh['data'=2,'dap'=4] {'dap'}, dimensions={1}, use_global_device_ids=true | all-gather | bytes 327680 | tf_op jit(solution)/shard_map/all_gather | solution.py:57
  101.9 10.9 %fusion.288 = (bf16[32,4,128,8,32]{2,4,3,1,0:T(8,128)(2,1)}, f32[32,4,128,8,32]{2,4,3,1,0:T(8,128)}) fusion(bf16[256,4,8,32]{0,3,2,1:T(8,128)(2,1)S(1)} %copy-done, f32[32,128]{1,0:T(8,128)S(1)} %add_rsqrt_fusion.8, f32[32,128]{1,0:T(8,128)S(1)} %get-tuple-element.256, bf16[2,32,128,256]{3,2,1,0:T(8,128)(2,1)} %param.17), kind=kOutput, calls=%fused_computation.416 | convolution fusion | flops 2155872256 | bytes 27820032 | tf_op jit(solution)/shard_map/while/body/eval_jaxpr/vmap(lc,cghd->glhd)/dot_general | solution.py:32
  112.8 12.4 %fusion.289 = (f32[32,8,128]{2,1,0:T(8,128)S(1)}, f32[32,8,128,128]{2,3,1,0:T(8,128)}) fusion(f32[8,128,128]{1,2,0:T(8,128)S(1)} %copy.145, f32[32,128]{1,0:T(8,128)S(1)} %multiply_bitcast_fusion.2, bf16[32,4,128,8,32]{2,4,3,1,0:T(8,128)(2,1)} %get-tuple-element.172), kind=kOutput, calls=%fused_computation.417 | convolution fusion | flops 289407104 | bytes 21643264 | tf_op jit(solution)/shard_map/while/body/eval_jaxpr/vmap()/sub | solution.py:41
  125.1 9.7 %fusion.57 = bf16[32,128,256]{2,1,0:T(8,128)(2,1)S(1)} fusion(bf16[2,32,128,256]{3,2,1,0:T(8,128)(2,1)} %param.17, f32[32,4,128,8,32]{2,4,3,1,0:T(8,128)} %get-tuple-element.173, f32[32,8,128,128]{2,3,1,0:T(8,128)} %get-tuple-element.175, f32[32,8,128]{2,1,0:T(8,128)S(1)} %get-tuple-element.174, bf16[32,4,128,8,32]{2,4,3,1,0:T(8,128)(2,1)} %get-tuple-element.172, ...), kind=kOutput, calls=%fused_computation.93 | convolution fusion | flops 822083584 | bytes 27525120 | tf_op jit(solution)/shard_map/while/body/eval_jaxpr/vmap(qhd,hdc->qc)/dot_general | solution.py:43
  150.8 7.1 %fusion.294 = (bf16[32,4,128,8,32]{2,4,3,1,0:T(8,128)(2,1)S(1)}, f32[32,4,128,8,32]{2,4,3,1,0:T(8,128)}) fusion(bf16[256,4,8,32]{0,3,2,1:T(8,128)(2,1)S(1)} %copy-done.18, bf16[32,128,256]{2,1,0:T(8,128)(2,1)S(1)} %multiply_convert_fusion.1), kind=kOutput, calls=%fused_computation.422 | convolution fusion | flops 2151677952 | bytes 27787264 | tf_op jit(solution)/shard_map/while/body/eval_jaxpr/vmap(lc,cghd->glhd)/dot_general | solution.py:32
  161.1 7.0 %fusion.155 = f32[32,8,128,128]{2,3,1,0:T(8,128)} fusion(bf16[32,4,128,8,32]{2,4,3,1,0:T(8,128)(2,1)S(1)} %get-tuple-element.199), kind=kOutput, calls=%fused_computation.227 | convolution fusion | flops 268435456 | bytes 20971520 | tf_op jit(solution)/shard_map/while/body/eval_jaxpr/vmap(qhd,khd->hqk)/dot_general | solution.py:38
  168.1 18.9 %fusion.295 = (f32[32,8,128]{2,1,0:T(8,128)S(1)}, f32[32,8,128,128]{2,3,1,0:T(8,128)}) fusion(f32[32,8,128,128]{2,3,1,0:T(8,128)} %fusion.155, f32[32,128]{1,0:T(8,128)S(1)} %copy.139), kind=kOutput, calls=%fused_computation.423 | output fusion | flops 25165952 | bytes 33701888 | tf_op jit(solution)/shard_map/while/body/eval_jaxpr/vmap()/sub | solution.py:41
  187.0 11.8 %convert_reduce_fusion.1 = (f32[32,128]{1,0:T(8,128)S(1)}, bf16[32,128,256]{2,1,0:T(8,128)(2,1)}) fusion(bf16[8,32,256]{2,1,0:T(8,128)(2,1)S(1)} %copy-done.32, f32[32,4,128,8,32]{2,4,3,1,0:T(8,128)} %get-tuple-element.200, f32[32,8,128,128]{2,3,1,0:T(8,128)} %get-tuple-element.202, f32[32,8,128]{2,1,0:T(8,128)S(1)} %get-tuple-element.201, ...), kind=kOutput, calls=%fused_computation.67 | convolution fusion | flops 823128064 | bytes 29638656 | tf_op jit(solution)/shard_map/while/body/eval_jaxpr/vmap(qhd,hdc->qc)/dot_general | solution.py:43
  210.0 7.1 %fusion.290 = (bf16[32,4,128,8,32]{2,4,3,1,0:T(8,128)(2,1)S(1)}, f32[32,4,128,8,32]{2,4,3,1,0:T(8,128)}) fusion(bf16[256,4,8,32]{0,3,2,1:T(8,128)(2,1)S(1)} %copy-done.18, bf16[32,128,256]{2,1,0:T(8,128)(2,1)S(1)} %multiply_convert_fusion), kind=kOutput, calls=%fused_computation.418 | convolution fusion | flops 2151677952 | bytes 27787264 | tf_op jit(solution)/shard_map/while/body/eval_jaxpr/vmap(lc,cghd->glhd)/dot_general | solution.py:32
  220.4 7.0 %fusion.154 = f32[32,8,128,128]{2,3,1,0:T(8,128)} fusion(bf16[32,4,128,8,32]{2,4,3,1,0:T(8,128)(2,1)S(1)} %get-tuple-element.184), kind=kOutput, calls=%fused_computation.220 | convolution fusion | flops 268435456 | bytes 20971520 | tf_op jit(solution)/shard_map/while/body/eval_jaxpr/vmap(qhd,khd->hqk)/dot_general | solution.py:38
  227.4 18.9 %fusion.291 = (f32[32,8,128]{2,1,0:T(8,128)S(1)}, f32[32,8,128,128]{2,3,1,0:T(8,128)}) fusion(f32[32,8,128,128]{2,3,1,0:T(8,128)} %fusion.154, f32[32,128]{1,0:T(8,128)S(1)} %copy.149), kind=kOutput, calls=%fused_computation.419 | output fusion | flops 25165952 | bytes 33701888 | tf_op jit(solution)/shard_map/while/body/eval_jaxpr/vmap()/sub | solution.py:41
  246.2 11.8 %convert_reduce_fusion = (f32[32,128]{1,0:T(8,128)S(1)}, bf16[32,128,256]{2,1,0:T(8,128)(2,1)}) fusion(bf16[8,32,256]{2,1,0:T(8,128)(2,1)S(1)} %copy-done.32, f32[32,4,128,8,32]{2,4,3,1,0:T(8,128)} %get-tuple-element.185, f32[32,8,128,128]{2,3,1,0:T(8,128)} %get-tuple-element.187, f32[32,8,128]{2,1,0:T(8,128)S(1)} %get-tuple-element.186, ...), kind=kOutput, calls=%fused_computation.65 | convolution fusion | flops 823128064 | bytes 29638656 | tf_op jit(solution)/shard_map/while/body/eval_jaxpr/vmap(qhd,hdc->qc)/dot_general | solution.py:43
  267.1 24.3 %fusion.210 = f32[128,32,32,32]{3,1,2,0:T(8,128)} fusion(bf16[128,128,32]{1,2,0:T(8,128)(2,1)} %all-gather.3.cloned.1.call-done, bf16[2,32,128,32]{2,3,0,1:T(8,128)(2,1)S(1)} %fusion.189, bf16[32,128]{1,0:T(8,128)(2,1)S(1)} %copy.154), kind=kOutput, calls=%fused_computation.304 | convolution fusion | flops 1074266112 | bytes 18096128 | tf_op jit(solution)/shard_map/while/body/eval_jaxpr/vmap(se,jsf->jef)/dot_general | solution.py:73
  291.4 51.9 %copy.155 = f32[128,32,32,32]{0,1,3,2:T(8,128)} copy(f32[128,32,32,32]{3,1,2,0:T(8,128)} %fusion.210) | data formatting | bytes 33554432 | tf_op jit(solution)/shard_map/while/body/eval_jaxpr/vmap(se,jsf->jef)/dot_general | solution.py:73
  343.4 7.5 %convert_reduce_fusion.5 = (f32[32,128]{1,0:T(8,128)S(1)}, bf16[32,128,128]{1,2,0:T(8,128)(2,1)S(1)}) fusion(bf16[32,32,128]{2,1,0:T(8,128)(2,1)S(1)} %copy-done.30, f32[128,32,32,32]{0,1,3,2:T(8,128)} %copy.155, f32[32,128]{1,0:T(8,128)S(1)} %copy-done.25, bf16[1,32,128,128]{2,3,1,0:T(8,128)(2,1)S(1)} %copy-done.10), kind=kOutput, calls=%fused_computation.160 | convolution fusion | flops 1084747776 | bytes 19169280 | tf_op jit(solution)/shard_map/while/body/eval_jaxpr/vmap(jef,efc->jc)/dot_general | solution.py:75
  357.5 24.3 %fusion.207 = f32[128,32,32,32]{3,1,2,0:T(8,128)} fusion(bf16[128,128,32]{1,2,0:T(8,128)(2,1)} %all-gather.5.cloned.1.call-done, bf16[2,32,128,32]{2,3,0,1:T(8,128)(2,1)S(1)} %copy-done.22, bf16[32,128]{1,0:T(8,128)(2,1)S(1)} %copy.171), kind=kOutput, calls=%fused_computation.301 | convolution fusion | flops 1074266112 | bytes 18096128 | tf_op jit(solution)/shard_map/while/body/eval_jaxpr/vmap(se,jsf->jef)/dot_general | solution.py:73
  381.8 52.2 %copy.172 = f32[128,32,32,32]{0,1,3,2:T(8,128)} copy(f32[128,32,32,32]{3,1,2,0:T(8,128)} %fusion.207) | data formatting | bytes 33554432 | tf_op jit(solution)/shard_map/while/body/eval_jaxpr/vmap(se,jsf->jef)/dot_general | solution.py:73
  434.0 7.4 %convert_reduce_fusion.4 = (f32[32,128]{1,0:T(8,128)S(1)}, bf16[32,128,128]{1,2,0:T(8,128)(2,1)S(1)}) fusion(bf16[32,32,128]{2,1,0:T(8,128)(2,1)S(1)} %copy-done.30, f32[128,32,32,32]{0,1,3,2:T(8,128)} %copy.172, f32[32,128]{1,0:T(8,128)S(1)} %copy-done.24, bf16[1,32,128,128]{2,3,1,0:T(8,128)(2,1)S(1)} %copy-done.12), kind=kOutput, calls=%fused_computation.157 | convolution fusion | flops 1084747776 | bytes 19169280 | tf_op jit(solution)/shard_map/while/body/eval_jaxpr/vmap(jef,efc->jc)/dot_general | solution.py:75
  442.2 6.2 fusion.296
  448.4 8.9 %all_gather.27 = bf16[4,128,128]{2,0,1:T(4,128)(2,1)S(1)} all-gather(bf16[4,32,128]{2,0,1:T(4,128)(2,1)S(1)} %fusion.194), channel_id=1, replica_groups=mesh['data'=2,'dap'=4] {'dap'}, dimensions={1}, use_global_device_ids=true | all-gather | bytes 163840 | tf_op jit(solution)/shard_map/all_gather | solution.py:57
  477.4 16.8 %all_gather.30 = bf16[4,128,128]{2,0,1:T(4,128)(2,1)S(1)} all-gather(bf16[4,32,128]{2,0,1:T(4,128)(2,1)S(1)} %fusion.196), channel_id=1, replica_groups=mesh['data'=2,'dap'=4] {'dap'}, dimensions={1}, use_global_device_ids=true | all-gather | bytes 163840 | tf_op jit(solution)/shard_map/all_gather | solution.py:57
  503.3 6.8 %fusion.127 = bf16[32,128,128]{1,2,0:T(8,128)(2,1)} fusion(bf16[32,128,128]{1,2,0:T(8,128)(2,1)S(1)} %copy-done.17, f32[32,4,128,4,32]{2,4,3,1,0:T(8,128)} %get-tuple-element.215, f32[32,4,128,128]{2,3,1,0:T(8,128)} %get-tuple-element.217, f32[32,4,128]{2,1,0:T(4,128)S(1)} %get-tuple-element.216, bf16[32,4,128,4,32]{2,4,3,1,0:T(8,128)(2,1)} %get-tuple-element.214, ...), kind=kOutput, calls=%fused_computation.190 | convolution fusion | flops 276824064 | bytes 13729792 | tf_op jit(solution)/shard_map/while/body/eval_jaxpr/vmap(qhd,hdc->qc)/dot_general | solution.py:43
  522.2 11.0 %all_gather.28 = bf16[4,128,128]{2,0,1:T(4,128)(2,1)S(1)} all-gather(bf16[4,32,128]{2,0,1:T(4,128)(2,1)S(1)} %fusion.195), channel_id=1, replica_groups=mesh['data'=2,'dap'=4] {'dap'}, dimensions={1}, use_global_device_ids=true | all-gather | bytes 163840 | tf_op jit(solution)/shard_map/all_gather | solution.py:57
  558.9 7.5 %fusion.157 = bf16[128,32,128]{2,0,1:T(8,128)(2,1)} fusion(f32[4,32,32,128]{3,1,0,2:T(8,128)} %copy-done.5, f32[32,4,128,4,32]{2,4,3,1,0:T(8,128)} %get-tuple-element.245, f32[32,4,128,128]{2,3,1,0:T(8,128)} %get-tuple-element.247, f32[32,4,128]{2,1,0:T(4,128)S(1)} %get-tuple-element.246, bf16[32,4,128,4,32]{2,4,3,1,0:T(8,128)(2,1)} %copy-done.8, ...), kind=kOutput, calls=%fused_computation.238 | convolution fusion | flops 276299776 | bytes 14778368 | tf_op jit(solution)/shard_map/while/body/eval_jaxpr/vmap(qhd,hdc->qc)/dot_general | solution.py:43
  572.5 6.1 fusion.298
  583.1 28.1 %all_gather.31 = bf16[4,128,128]{2,0,1:T(4,128)(2,1)S(1)} all-gather(bf16[4,32,128]{2,0,1:T(4,128)(2,1)S(1)} %fusion.197), channel_id=1, replica_groups=mesh['data'=2,'dap'=4] {'dap'}, dimensions={1}, use_global_device_ids=true | all-gather | bytes 163840 | tf_op jit(solution)/shard_map/all_gather | solution.py:57
  624.4 6.8 %fusion.156 = bf16[128,32,128]{2,0,1:T(8,128)(2,1)} fusion(f32[4,32,32,128]{3,1,0,2:T(8,128)S(1)} %copy.181, f32[32,4,128,4,32]{2,4,3,1,0:T(8,128)} %get-tuple-element.226, f32[32,4,128,128]{2,3,1,0:T(8,128)} %get-tuple-element.228, f32[32,4,128]{2,1,0:T(4,128)S(1)} %get-tuple-element.227, bf16[32,4,128,4,32]{2,4,3,1,0:T(8,128)(2,1)} %get-tuple-element.218, ...), kind=kOutput, calls=%fused_computation.235 | convolution fusion | flops 276299776 | bytes 14778368 | tf_op jit(solution)/shard_map/while/body/eval_jaxpr/vmap(qhd,hdc->qc)/dot_general | solution.py:43
  649.4 6.9 %all-to-all-done.7 = bf16[128,32,128]{2,1,0:T(8,128)(2,1)S(1)} async-done(((bf16[128,32,128]{2,1,0:T(8,128)(2,1)}), bf16[128,32,128]{2,1,0:T(8,128)(2,1)S(1)}, u32[]{:S(2)}, u32[]{:S(2)}) %all-to-all-start.7) | async-done | bytes 1048608 | tf_op jit(solution)/shard_map/all_to_all | solution.py:103
  (210 shorter events, 182.2 us)
Async XLA Ops:
  7.2 22.6 %copy-start = (bf16[256,4,8,32]{0,3,2,1:T(8,128)(2,1)S(1)}, bf16[256,4,8,32]{0,3,2,1:T(8,128)(2,1)}, u32[]{:S(2)}) copy-start(bf16[256,4,8,32]{0,3,2,1:T(8,128)(2,1)} %param.22) | copy-start | bytes 1572868
  11.6 15.5 %copy-start.9 = (bf16[1,32,128,128]{2,3,1,0:T(8,128)(2,1)}, bf16[1,32,128,128]{2,3,1,0:T(8,128)(2,1)S(1)}, u32[]{:S(2)}) copy-start(bf16[1,32,128,128]{2,3,1,0:T(8,128)(2,1)S(1)} %copy.227) | copy-start | bytes 3145732
  23.5 6.2 copy-start.23
  40.7 12.4 %copy-start.31 = (bf16[8,32,256]{2,1,0:T(8,128)(2,1)S(1)}, bf16[8,32,256]{2,1,0:T(8,128)(2,1)}, u32[]{:S(2)}) copy-start(bf16[8,32,256]{2,1,0:T(8,128)(2,1)} %param.23) | copy-start | bytes 393220
  68.2 72.0 %all-to-all-start = ((bf16[32,128,256]{2,0,1:T(8,128)(2,1)}), bf16[32,128,256]{2,0,1:T(8,128)(2,1)}, u32[]{:S(2)}, u32[]{:S(2)}) async-start(bf16[32,128,256]{2,0,1:T(8,128)(2,1)} %copy.137), calls=%async_computation | async-start | bytes 4194304 | tf_op jit(solution)/shard_map/all_to_all | solution.py:90
  73.6 39.2 %copy-start.11 = (bf16[1,32,128,128]{2,3,1,0:T(8,128)(2,1)}, bf16[1,32,128,128]{2,3,1,0:T(8,128)(2,1)S(1)}, u32[]{:S(2)}) copy-start(bf16[1,32,128,128]{2,3,1,0:T(8,128)(2,1)S(1)} %copy.228) | copy-start | bytes 3145732
  140.2 64.9 %all-to-all-start.2 = ((bf16[32,128,256]{2,0,1:T(8,128)(2,1)}), bf16[32,128,256]{2,0,1:T(8,128)(2,1)S(1)}, u32[]{:S(2)}, u32[]{:S(2)}) async-start(bf16[32,128,256]{2,0,1:T(8,128)(2,1)} %copy.147), calls=%async_computation.2 | async-start | bytes 4194304 | tf_op jit(solution)/shard_map/all_to_all | solution.py:90
  143.8 123.3 %all-gather.3.cloned.1.call-start = ((), (), s32[]{:S(2)}) async-start(), calls=%async_computation.8 | async-start | bytes 1310720 | tf_op jit(solution)/shard_map/all_gather | solution.py:97
  168.1 18.9 %copy-start.32 = (bf16[8,32,256]{2,1,0:T(8,128)(2,1)S(1)}, bf16[8,32,256]{2,1,0:T(8,128)(2,1)}, u32[]{:S(2)}) copy-start(bf16[8,32,256]{2,1,0:T(8,128)(2,1)} %param.25) | copy-start | bytes 393220
  187.0 14.3 %copy-start.33 = (bf16[256,2,32]{0,2,1:T(8,128)(2,1)S(1)}, bf16[256,2,32]{0,2,1:T(8,128)(2,1)}, u32[]{:S(2)}) copy-start(bf16[256,2,32]{0,2,1:T(8,128)(2,1)} %param.26) | copy-start | bytes 98308
  204.9 152.6 %all-gather.5.cloned.1.call-start = ((), (), s32[]{:S(2)}) async-start(), calls=%async_computation.9 | async-start | bytes 1310720 | tf_op jit(solution)/shard_map/all_gather | solution.py:97
  246.2 11.8 %copy-start.14 = (bf16[32,128,256]{2,1,0:T(8,128)(2,1)S(1)}, bf16[32,128,256]{2,1,0:T(8,128)(2,1)}, u32[]{:S(2)}) copy-start(bf16[32,128,256]{2,1,0:T(8,128)(2,1)} %get-tuple-element.230) | copy-start | bytes 6291460
  266.3 25.1 %copy-start.21 = (bf16[2,32,128,32]{2,3,0,1:T(8,128)(2,1)}, bf16[2,32,128,32]{2,3,0,1:T(8,128)(2,1)S(1)}, u32[]{:S(2)}) copy-start(bf16[2,32,128,32]{2,3,0,1:T(8,128)(2,1)S(1)} %fusion.186) | copy-start | bytes 1572868
  291.4 52.0 %copy-start.10 = (bf16[1,32,128,128]{2,3,1,0:T(8,128)(2,1)S(1)}, bf16[1,32,128,128]{2,3,1,0:T(8,128)(2,1)}, u32[]{:S(2)}) copy-start(bf16[1,32,128,128]{2,3,1,0:T(8,128)(2,1)} %copy-done.9) | copy-start | bytes 3145732
  291.4 52.0 %copy-start.25 = (f32[32,128]{1,0:T(8,128)S(1)}, f32[32,128]{1,0:T(8,128)}, u32[]{:S(2)}) copy-start(f32[32,128]{1,0:T(8,128)} %convolution_add_fusion.1) | copy-start | bytes 49156
  291.4 52.0 %copy-start.30 = (bf16[32,32,128]{2,1,0:T(8,128)(2,1)S(1)}, bf16[32,32,128]{2,1,0:T(8,128)(2,1)}, u32[]{:S(2)}) copy-start(bf16[32,32,128]{2,1,0:T(8,128)(2,1)} %param.27) | copy-start | bytes 786436
  343.4 7.9 %copy-start.37 = (bf16[128,4]{0,1:T(4,128)(2,1)S(1)}, bf16[128,4]{0,1:T(4,128)(2,1)}, u32[]{:S(2)}) copy-start(bf16[128,4]{0,1:T(4,128)(2,1)} %param.28) | copy-start | bytes 3076
  343.4 8.2 %copy-start.19 = (bf16[128,4,4,32]{0,3,2,1:T(8,128)(2,1)S(1)}, bf16[128,4,4,32]{0,3,2,1:T(8,128)(2,1)}, u32[]{:S(2)}) copy-start(bf16[128,4,4,32]{0,3,2,1:T(8,128)(2,1)} %param.29) | copy-start | bytes 393220
  381.8 52.2 %copy-start.12 = (bf16[1,32,128,128]{2,3,1,0:T(8,128)(2,1)S(1)}, bf16[1,32,128,128]{2,3,1,0:T(8,128)(2,1)}, u32[]{:S(2)}) copy-start(bf16[1,32,128,128]{2,3,1,0:T(8,128)(2,1)} %copy-done.11) | copy-start | bytes 3145732
  381.8 52.2 %copy-start.24 = (f32[32,128]{1,0:T(8,128)S(1)}, f32[32,128]{1,0:T(8,128)}, u32[]{:S(2)}) copy-start(f32[32,128]{1,0:T(8,128)} %convolution_add_fusion) | copy-start | bytes 49156
  441.4 6.9 %copy-start.16 = (bf16[32,128,128]{1,2,0:T(8,128)(2,1)}, bf16[32,128,128]{1,2,0:T(8,128)(2,1)S(1)}, u32[]{:S(2)}) copy-start(bf16[32,128,128]{1,2,0:T(8,128)(2,1)S(1)} %get-tuple-element.213) | copy-start | bytes 3145732
  460.3 6.0 copy-start.34
  473.9 38.9 %all-to-all-start.4 = ((bf16[32,128,128]{2,0,1:T(8,128)(2,1)}), bf16[32,128,128]{2,0,1:T(8,128)(2,1)S(1)}, u32[]{:S(2)}, u32[]{:S(2)}) async-start(bf16[32,128,128]{2,0,1:T(8,128)(2,1)} %copy.162), calls=%async_computation.4 | async-start | bytes 2097152 | tf_op jit(solution)/shard_map/all_to_all | solution.py:101
  497.3 6.0 copy-start.17
  512.8 31.6 %all-to-all-start.6 = ((bf16[32,128,128]{2,0,1:T(8,128)(2,1)}), bf16[32,128,128]{2,0,1:T(8,128)(2,1)S(1)}, u32[]{:S(2)}, u32[]{:S(2)}) async-start(bf16[32,128,128]{2,0,1:T(8,128)(2,1)} %copy.179), calls=%async_computation.6 | async-start | bytes 2097152 | tf_op jit(solution)/shard_map/all_to_all | solution.py:101
  518.9 14.4 %copy-start.20 = (bf16[128,4,4,32]{0,3,2,1:T(8,128)(2,1)S(1)}, bf16[128,4,4,32]{0,3,2,1:T(8,128)(2,1)}, u32[]{:S(2)}) copy-start(bf16[128,4,4,32]{0,3,2,1:T(8,128)(2,1)} %param.32) | copy-start | bytes 393220
  544.4 34.2 %all-to-all-start.1 = ((bf16[32,128,256]{2,0,1:T(8,128)(2,1)}), bf16[32,128,256]{2,0,1:T(8,128)(2,1)}, u32[]{:S(2)}, u32[]{:S(2)}) async-start(bf16[32,128,256]{2,0,1:T(8,128)(2,1)} %copy.141), calls=%async_computation.1 | async-start | bytes 4194304 | tf_op jit(solution)/shard_map/all_to_all | solution.py:104
  552.9 6.0 copy-start.35
  578.6 41.5 %all-to-all-start.3 = ((bf16[32,128,256]{2,0,1:T(8,128)(2,1)}), bf16[32,128,256]{2,0,1:T(8,128)(2,1)}, u32[]{:S(2)}, u32[]{:S(2)}) async-start(bf16[32,128,256]{2,0,1:T(8,128)(2,1)} %copy.151), calls=%async_computation.3 | async-start | bytes 4194304 | tf_op jit(solution)/shard_map/all_to_all | solution.py:104
  620.1 18.4 %all-to-all-start.5 = ((bf16[128,32,128]{2,1,0:T(8,128)(2,1)}), bf16[128,32,128]{2,1,0:T(8,128)(2,1)}, u32[]{:S(2)}, u32[]{:S(2)}) async-start(bf16[128,32,128]{2,1,0:T(8,128)(2,1)} %copy.168), calls=%async_computation.5 | async-start | bytes 2097152 | tf_op jit(solution)/shard_map/all_to_all | solution.py:103
  638.6 17.7 %all-to-all-start.7 = ((bf16[128,32,128]{2,1,0:T(8,128)(2,1)}), bf16[128,32,128]{2,1,0:T(8,128)(2,1)S(1)}, u32[]{:S(2)}, u32[]{:S(2)}) async-start(bf16[128,32,128]{2,1,0:T(8,128)(2,1)} %copy.185), calls=%async_computation.7 | async-start | bytes 2097152 | tf_op jit(solution)/shard_map/all_to_all | solution.py:103
  648.0 9.9 %copy-start.1 = (bf16[256,4,8,32]{0,3,2,1:T(8,128)(2,1)S(1)}, bf16[256,4,8,32]{0,3,2,1:T(8,128)(2,1)}, u32[]{:S(2)}) copy-start(bf16[256,4,8,32]{0,3,2,1:T(8,128)(2,1)} %param.22) | copy-start | bytes 1572868
  (16 other events, 52.0 us)
Sparse Core Ops, SparseCore 0:
  205.0 15.1 all-gather.2
  267.2 15.1 all-gather.4
where the time goes:
time: 677 us; the launch traced here: 665 us
  matrix products  254 us (38%)
  local copies, waits for them, and re-layouts  153 us (23%)
  blocking collectives  103 us (15%)
  other arithmetic  96.2 us (14%)
  starting transfers between devices  32.9 us (5%)
  between operations  15.5 us (2%)
  waiting for transfers between devices  11.4 us (2%)
    dot_general x2, local copies, waits for them, and re-layouts, one_row(): jnp.einsum('se,jsf->jef', left_row, right_proj, preferred_element_type=jn...  104 us
    all_gather x6, blocking collectives, gathered_bias(): return lax.all_gather(bias_part, GROUP_AXIS, axis=1, tiled=True)  103 us
    dot_general x8, matrix products, gated_attention(): jnp.einsum('qhd,hdc->qc', mixed.astype(jnp.bfloat16), w_out, preferred_el...  71.3 us
    sub x6, other arithmetic, gated_attention(): attn_prob = jax.nn.softmax(logits, axis=-1).astype(jnp.bfloat16)  61.7 us
    dot_general x8, matrix products, gated_attention(): jnp.einsum('lc,cghd->glhd', normed, w_qkvg, preferred_element_type=jnp.fl...  58.8 us
    dot_general x2, matrix products, one_row(): jnp.einsum('se,jsf->jef', left_row, right_proj, preferred_element_type=jn...  48.6 us
    dot_general x6, matrix products, gated_attention(): jnp.einsum('qhd,khd->hqk', queries, keys_bf, preferred_element_type=jnp.f...  27.1 us
    convert_element_type x12, local copies, waits for them, and re-layouts, gated_attention(): return (x_row.astype(jnp.float32) + update).astype(jnp.bfloat16)  26.8 us
  transfers between devices with their start and end apart: 10, of which 2 were waited for; matrix products, arithmetic and copies ran while one was open for 50% of the time, Pallas kernels for 0%

commit v1 on v0

v1 whole, which is shorter than its diff:
```python
import functools

import jax
import jax.numpy as jnp
from jax import lax
from jax.experimental import pallas as pl
from jax.experimental.pallas import tpu as pltpu
from jax.sharding import PartitionSpec as P

F32 = jnp.float32
BF16 = jnp.bfloat16
MASK_SCALE = 10000.0
LN_EPS = 1e-5
OPM_EPS = 1e-3
LOG2E = 1.4426950408889634
HEAD_DIM = 32
N = 128
B = 32
W = 256
K1 = 1024
COL_PITCH = 40
TRI_PITCH = 24
SCALE2 = (HEAD_DIM ** -0.5) * LOG2E
PART_AXIS = 'data'
GROUP_AXIS = 'dap'
MESH_ID = pl.DeviceIdType.MESH
NT = (((1,), (1,)), ((), ()))
NN = (((1,), (0,)), ((), ()))
TN = (((0,), (0,)), ((), ()))


def mm(lhs, rhs, dims):
    return lax.dot_general(lhs, rhs, dims, preferred_element_type=F32)


def layer_norm(xf):
    mean = jnp.mean(xf, axis=-1, keepdims=True)
    cen = xf - mean
    var = jnp.mean(cen * cen, axis=-1, keepdims=True)
    return (cen * lax.rsqrt(var + LN_EPS)).astype(BF16)


class Attention:
    def __init__(self, st, wt_ref, wo_ref, n_heads, load_x, bias_of, mask_of, emit, post=None):
        self.qs, self.ks, self.vs, self.gs, self.lg, self.mx, self.os = st
        self.wt, self.wo, self.n_heads, self.hd = wt_ref, wo_ref, n_heads, n_heads * HEAD_DIM
        self.load_x, self.bias_of, self.mask_of, self.emit, self.post = load_x, bias_of, mask_of, emit, post
        self.items = [(u, h) for u in range(2) for h in range(0, n_heads, 2)]

    def p_part(self, y, i, part):
        hd = self.hd
        w = self.wt[part * hd:(part + 1) * hd]
        if part == 0:
            self.qs[i % 2, 0:hd] = mm(w, y, NT).astype(BF16)
        elif part == 1:
            self.ks[i % 2, :, 0:hd] = mm(y, w, NT).astype(BF16)
        elif part == 2:
            self.vs[i % 4, 0:hd] = mm(w, y, NT).astype(BF16)
        else:
            self.gs[i % 4, 0:hd] = jax.nn.sigmoid(mm(w, y, NT))

    def l_part(self, p, i, item):
        u, h = item
        tok = slice(N * u, N * u + N)
        blocks = []
        for hh in (h, h + 1):
            h4 = hh % 4
            rows = [self.qs[i % 2, B * hh:B * hh + B, tok]]
            if h4 > 0:
                rows.insert(0, jnp.zeros((B * h4, N), BF16))
            if h4 < 3:
                rows.append(jnp.zeros((N - B - B * h4, N), BF16))
            blocks.append(jnp.concatenate(rows, axis=0))
        g0 = h // 4 * N
        logits = mm(self.ks[i % 2, tok, g0:g0 + N], jnp.concatenate(blocks, axis=1), NN)
        mask_col = self.mask_of(p, u)
        for n, hh in enumerate((h, h + 1)):
            lg = logits[:, N * n:N * n + N] * SCALE2
            bias = self.bias_of(hh)
            if bias is not None:
                lg = lg + bias
            if mask_col is not None:
                lg = lg + mask_col
            row = u * self.n_heads + hh
            self.lg[i % 2, row] = lg
            self.mx[i % 2, row:row + 1] = jnp.max(lg, axis=0, keepdims=True)

    def s_part(self, i, item):
        u, h = item
        tok = slice(N * u, N * u + N)
        ps, inv = [], []
        for hh in (h, h + 1):
            row = u * self.n_heads + hh
            ex = jnp.exp2(self.lg[i % 2, row] - self.mx[i % 2, row:row + 1])
            inv.append(1.0 / jnp.sum(ex, axis=0, keepdims=True))
            ps.append(ex.astype(BF16))
        h0 = h * B
        ov = mm(self.vs[i % 4, h0:h0 + 2 * B, tok], jnp.concatenate(ps, axis=1), NN)
        o = jnp.concatenate([ov[0:B, 0:N] * inv[0], ov[B:2 * B, N:W] * inv[1]], axis=0)
        self.os[i % 2, h0:h0 + 2 * B, tok] = (o * self.gs[i % 4, h0:h0 + 2 * B, tok]).astype(BF16)

    def o_part(self, p, i):
        self.emit(p, i % 2, self.load_x(p) + mm(self.os[i % 2, 0:self.hd], self.wo[...], TN))

    def step(self, p, i, last):
        if self.post is not None:
            self.post(jnp.maximum(p - 2, 0), i % 2)
        self.o_part(jnp.maximum(p - 1, 0), i - 1)
        y = layer_norm(self.load_x(jnp.minimum(p + 2, last)))
        nxt = jnp.minimum(p + 1, last)
        for n, item in enumerate(self.items):
            self.l_part(nxt, i + 1, item)
            self.s_part(i, item)
            for part in range(4):
                if part * len(self.items) // 4 == n:
                    self.p_part(y, i + 2, part)

    def begin(self):
        for i in range(2):
            y = layer_norm(self.load_x(i))
            for part in range(4):
                self.p_part(y, i, part)
        for item in self.items:
            self.l_part(0, 0, item)

    def end(self, last):
        self.o_part(last, 3)
        if self.post is not None:
            self.post(last - 1, 0)
            self.post(last, 1)


def rows_at(start, size):
    return pl.ds(pl.multiple_of(start, size), size)


def side_by_side(b):
    return jnp.concatenate([b[:, :N], b[:, N:]], axis=0)


def mega(m_in, z_in, mask_ref, mrow_ref, mcol_ref, mres_ref, w_rb, w_tsb, w_teb, w_row, w_row_o, w_col, w_col_o, w_ac, w_oo,
         w_ts, w_ts_o, w_te, w_te_o, m_out, z_out,
         zr, zot, ms, xx, rs, bb, bbf, bt, xf0, xf1, of0, of1, mo, at, ctx, ctf, cp, ninv, mtr, woot, rr,
         bs, bts, be, bte, zx, zs, zf, zof, zo, qs, ks, vs, gs, lgs, mxs, ots, nw, wtsb, wteb,
         l_sem, mi_s, mi_r, zi_s, zi_r, b_s, b_r, x_s, x_r, mo_s, mo_r, mo_l, c_s, c_r, bs_s, bs_r, be_s, be_r,
         zx_s, zx_r, zo_s, zo_r, zo_l):
    st = (qs, ks, vs, gs, lgs, mxs, ots)
    dat = lax.axis_index(PART_AXIS)
    dev = lax.axis_index(GROUP_AXIS)
    x = dev // 2
    c = dev % 2
    ox = 1 - x

    def peer(flip):
        px = ox if flip >= 2 else x
        pc = (1 - c) if flip % 2 else c
        return px * 2 + pc

    def remote(src, dst, s_sem, r_sem, flip):
        return pltpu.make_async_remote_copy(src, dst, s_sem, r_sem, device_id=(dat, peer(flip)),
                                            device_id_type=MESH_ID)

    barrier = pltpu.get_barrier_semaphore()
    for flip in (1, 2, 3):
        pl.semaphore_signal(barrier, inc=1, device_id=(dat, peer(flip)), device_id_type=MESH_ID)
    cp_zo = pltpu.make_async_copy(z_in.at[ox], zot, l_sem.at[0])
    cp_zr = pltpu.make_async_copy(z_in.at[x], zr.at[x], l_sem.at[1])
    cp_m = pltpu.make_async_copy(m_in.at[x], ms.at[x], l_sem.at[2])
    cp_zo.start()
    cp_zr.start()
    cp_m.start()
    pl.semaphore_wait(barrier, 3)

    def m_chunk(j):
        return remote(m_in.at[ox, pl.ds(4 * j, 4)], ms.at[x, pl.ds(4 * j, 4)], mi_s.at[j], mi_r.at[j], 2)

    m_chunk(0).start()

    def bias_rows(load, base):
        def body(g, carry):
            for p in range(4):
                y = layer_norm(load(8 * g + 2 * p).reshape(W, N).astype(F32))
                b = side_by_side(mm(w_rb[...], y, NT)).astype(BF16)
                bb[rows_at(base + 64 * g + 16 * p, 16)] = b
            return carry
        lax.fori_loop(0, 4, body, 0)

    row0 = pl.multiple_of(dev * W, W)
    spare = K1
    cp_zo.wait()
    bias_rows(lambda r: zot[pl.ds(r, 2)], spare)
    b_copies = []
    for n, flip in enumerate((2, 3)):
        b_copies.append(remote(bb.at[pl.ds(spare, W)], bb.at[pl.ds(row0, W)], b_s.at[n], b_r.at[n], flip))
    for cpy in b_copies:
        cpy.start()
    for j in range(1, 8):
        m_chunk(j).start()
    z_copy = remote(z_in.at[ox], zr.at[x], zi_s.at[0], zi_r.at[0], 2)
    z_copy.start()
    cp_zr.wait()

    bias_rows(lambda r: zr[x, pl.ds(r, 2)], row0)
    b_own = remote(bb.at[pl.ds(row0, W)], bb.at[pl.ds(row0, W)], b_s.at[2], b_r.at[2], 1)
    b_own.start()
    b_copies.append(b_own)

    for wdst, wsrc in ((wtsb, w_tsb), (wteb, w_teb)):
        wdst[0:4] = wsrc[...].astype(F32)
        wdst[4:8] = jnp.zeros((4, N), F32)
    mk = mask_ref[x].astype(F32)
    mkb = mk.astype(BF16)
    ninv[...] = 1.0 / (mm(mkb, mkb, TN) + OPM_EPS)
    mtr[...] = jnp.transpose(mk)
    for e in range(B):
        ctf[pl.ds(e * COL_PITCH, B)] = w_oo[B * e:B * e + B].astype(F32)
    def perm_oo(f, carry):
        xf0[rows_at(B * f, B)] = ctf[pl.ds(f, B, stride=COL_PITCH), :]
        return carry
    lax.fori_loop(0, B, perm_oo, 0)
    for t in range(8):
        woot[:, N * t:N * t + N] = jnp.transpose(xf0[N * t:N * t + N, :]).astype(BF16)

    for cpy in b_copies:
        cpy.wait_recv()
    bbf[...] = bb[0:K1].astype(F32) * LOG2E
    for h in range(8):
        bt[h] = jnp.transpose(bbf[pl.ds(h, N, stride=8), :])

    cp_m.wait()

    def x_chunk(ch):
        k = jnp.where(ch < 4, x, ox)
        rows = rows_at(k * B + (ch % 4) * 8, 8)
        return remote(rs.at[rows], xx.at[c, rows], x_s.at[ch], x_r.at[ch], 1)

    def row_seq(p):
        return jnp.where(p < 16, x, ox) * B + 2 * (p % 16)

    def row_x(p):
        s = row_seq(p)
        return ms[s // B, pl.ds(s % B, 2)].reshape(W, W).astype(F32)

    def lane_mask(ref, row, u):
        return jnp.broadcast_to(ref[row][:, u:u + 1], (N, N))

    def row_emit(p, slot, new):
        s = row_seq(p)
        new = new.reshape(2, 2, 2, B, W)
        even, odd = new[:, :, 0], new[:, :, 1]
        xx[c, pl.ds(s, 2)] = jnp.where(c == 0, even, odd).astype(BF16)
        rs[pl.ds(s, 2)] = jnp.where(c == 0, odd, even).astype(BF16)

    row = Attention(st, w_row, w_row_o, 8, row_x, lambda h: bt[h],
                    lambda p, u: lane_mask(mrow_ref, row_seq(p) // 2, u), row_emit)

    def row_four(t, carry):
        @pl.when(jnp.logical_and(t >= 3, t < 7))
        def _():
            m_chunk(2 * t - 6).wait_recv()
            m_chunk(2 * t - 5).wait_recv()

        for e in range(4):
            row.step(4 * t + e, e, 31)

        @pl.when(t > 0)
        def _():
            x_chunk(t - 1).start()
        return carry
    row.begin()
    lax.fori_loop(0, 8, row_four, 0)
    row.end(31)
    x_chunk(7).start()

    def x_wait(ch, carry):
        x_chunk(ch).wait_recv()
        return carry
    lax.fori_loop(0, 8, x_wait, 0)

    def mo_copies(q):
        out = []
        res0 = pl.multiple_of((2 * q + c) * B, B)
        for flip in range(4):
            src = mo.at[pl.ds(peer(flip) * B, B), q]
            dst = m_out.at[x, :, pl.ds(res0, B)]
            if flip == 0:
                out.append(pltpu.make_async_copy(src, dst, mo_l.at[q]))
            else:
                out.append(remote(src, dst, mo_s.at[q, flip - 1], mo_r.at[q, flip - 1], flip))
        return out

    def c_copy(q):
        rows = rows_at((2 * q + c) * K1, K1)
        return remote(ctx.at[rows], ctx.at[rows], c_s.at[q], c_r.at[q], 1)

    def col_x(p):
        return jnp.concatenate([
            jnp.concatenate([ref[pl.ds(2 * p + u, N, stride=COL_PITCH), :] for ref in (xf0, xf1)], axis=1)
            for u in range(2)], axis=0)

    def col_chunk(q, carry):
        for c2 in range(2):
            for k in range(2):
                for r in range(B):
                    v = xx[c2, k * B + r, q].astype(F32)
                    rows = pl.ds(((2 * k + c2) * B + r) * COL_PITCH, B)
                    xf0[rows] = v[:, :N]
                    xf1[rows] = v[:, N:]

        def col_post(p, slot):
            ac = mm(w_ac[...], layer_norm(nw[slot].astype(F32)), NT).astype(BF16).astype(F32)
            for u in range(2):
                loc = q * B + 2 * p + u
                nat = (2 * q + c) * B + 2 * p + u
                acm = (ac[:, N * u:N * u + N] * mtr[pl.ds(nat, 1), :]).astype(BF16)
                at[rows_at(loc * B, B)] = acm[0:B]
                ctx[rows_at(nat * B, B)] = acm[B:2 * B]

        def col_emit(p, slot, new):
            nw[slot] = new.astype(BF16)
            for u in range(2):
                of0[pl.ds(2 * p + u, N, stride=COL_PITCH), :] = new[N * u:N * u + N, :N]
                of1[pl.ds(2 * p + u, N, stride=COL_PITCH), :] = new[N * u:N * u + N, N:]

        col = Attention(st, w_col, w_col_o, 8, col_x, lambda h: None,
                        lambda p, u: lane_mask(mcol_ref, q * 16 + p, u), col_emit, col_post)

        def col_four(t, carry2):
            for e in range(4):
                col.step(4 * t + e, e, 15)
            return carry2
        col.begin()
        lax.fori_loop(0, 4, col_four, 0)
        col.end(15)
        for r in range(N):
            rows = pl.ds(r * COL_PITCH, B)
            mo[r, q] = jnp.concatenate([of0[rows, :], of1[rows, :]], axis=1).astype(BF16)
        c_copy(q).start()
        for cpy in mo_copies(q):
            cpy.start()
        return carry
    lax.fori_loop(0, 2, col_chunk, 0)

    for q in range(2):
        c_copy(q).wait_recv()
    for j in range(N):
        ctf[pl.ds(j * COL_PITCH, B)] = ctx[B * j:B * j + B].astype(F32)

    def perm_c(f, carry):
        cp[rows_at(f * N, N)] = ctf[pl.ds(f, N, stride=COL_PITCH), :].astype(BF16)
        return carry
    lax.fori_loop(0, B, perm_c, 0)
    z_copy.wait_recv()

    def opm_place(ib):
        k, r0 = ib // 4, (ib % 4) * 8
        return k, r0, (2 * k + c) * B + r0

    def opm_outer(ib, slot, fp):
        nat0 = opm_place(ib)[2]
        o = mm(at[rows_at(ib * W, W)], cp[fp * W:fp * W + W], NT)
        for i in range(8):
            nrow = ninv[pl.ds(nat0 + i, 1), :]
            for ff in range(2):
                blk = o[B * i:B * i + B, N * ff:N * ff + N] * nrow
                rr[slot, i, fp * 64 + B * ff:fp * 64 + B * ff + B] = blk.astype(BF16)

    def opm_load(ib, ip):
        k, r0, _ = opm_place(ib)
        return zr[k, pl.ds(r0 + 2 * ip, 2)].reshape(W, N).astype(F32)

    def opm_update(z_old, slot, ip):
        upd_t = mm(woot[...], jnp.concatenate([rr[slot, 2 * ip], rr[slot, 2 * ip + 1]], axis=1), NN)
        zn = (z_old + jnp.concatenate([jnp.transpose(upd_t[:, :N]), jnp.transpose(upd_t[:, N:])], axis=0)).astype(BF16)
        b = side_by_side(mm(wtsb[...].astype(BF16), layer_norm(zn.astype(F32)), NT)).astype(BF16).astype(F32)
        return zn, b

    def opm_store(ib, ip, zn, b):
        k, r0, nat0 = opm_place(ib)
        zr[k, pl.ds(r0 + 2 * ip, 2)] = zn.reshape(2, N, N)
        bs[rows_at((nat0 + 2 * ip) * 8, 16)] = b

    def opm_two(t, carry):
        for e in range(2):
            ib = 2 * t + e
            nxt = jnp.minimum(ib + 1, 7)
            olds = [opm_load(ib, ip) for ip in range(4)]
            news = []
            for ip in range(4):
                for fp in range(4):
                    opm_outer(nxt, 1 - e, ip * 4 + fp)
                news.append(opm_update(olds[ip], e, ip))
            for ip in range(4):
                opm_store(ib, ip, *news[ip])
        return carry
    for fp in range(16):
        opm_outer(0, 0, fp)
    lax.fori_loop(0, 4, opm_two, 0)

    def tri_bias_copies(ref, s_sem, r_sem):
        out = []
        for k in range(2):
            rows = rows_at((2 * k + c) * W, W)
            out.append(remote(ref.at[rows], ref.at[rows], s_sem.at[k], r_sem.at[k], 1))
        return out
    bs_copies = tri_bias_copies(bs, bs_s, bs_r)
    for cpy in bs_copies:
        cpy.start()
    for cpy in bs_copies:
        cpy.wait_recv()
    mres = jnp.broadcast_to(mres_ref[...], (N, N))
    for h in range(4):
        bts[h] = jnp.transpose(bs[pl.ds(h, N, stride=8), :]) * LOG2E + mres

    def zx_copy(ob):
        rows = rows_at(ob * 8, 8)
        return remote(zs.at[rows], zx.at[c, rows], zx_s.at[ob], zx_r.at[ob], 1)

    def ts_x(p):
        return zr[p // 16, pl.ds(2 * (p % 16), 2)].reshape(W, N).astype(F32)

    def ts_post(p, slot):
        b = mm(wteb[...].astype(BF16), layer_norm(nw[slot, :, 0:N].astype(F32)), NT)
        nat = (2 * (p // 16) + c) * B + 2 * (p % 16)
        be[rows_at(nat * 8, 16)] = side_by_side(b).astype(BF16).astype(F32)

    def ts_emit(p, slot, new):
        nw[slot, :, 0:N] = new.astype(BF16)
        new = new.reshape(2, 2, 2, B, N)
        even, odd = new[:, :, 0], new[:, :, 1]
        zx[c, pl.ds(2 * p, 2)] = jnp.where(c == 0, even, odd).astype(BF16)
        zs[pl.ds(2 * p, 2)] = jnp.where(c == 0, odd, even).astype(BF16)

    ts = Attention(st, w_ts, w_ts_o, 4, ts_x, lambda h: bts[h], lambda p, u: None, ts_emit, ts_post)

    def ts_four(ob, carry):
        for e in range(4):
            ts.step(4 * ob + e, e, 31)

        @pl.when(ob > 0)
        def _():
            zx_copy(ob - 1).start()
        return carry
    ts.begin()
    lax.fori_loop(0, 8, ts_four, 0)
    ts.end(31)
    zx_copy(7).start()
    be_copies = tri_bias_copies(be, be_s, be_r)
    for cpy in be_copies:
        cpy.start()
    for cpy in be_copies:
        cpy.wait_recv()
    for h in range(4):
        bte[h] = be[pl.ds(h, N, stride=8), :] * LOG2E + mres

    def zx_wait(ob, carry):
        zx_copy(ob).wait_recv()
        return carry
    lax.fori_loop(0, 8, zx_wait, 0)

    def zo_copies(ci, q, hf):
        out = []
        col0 = pl.multiple_of((2 * q + c) * B + hf * 16, 16)
        h16 = pl.multiple_of(hf * 16, 16)
        for flip in range(4):
            home = peer(flip)
            src = zo.at[pl.ds(home * B, B), q, pl.ds(h16, 16)]
            dst = z_out.at[x, :, pl.ds(col0, 16)]
            if flip == 0:
                out.append(pltpu.make_async_copy(src, dst, zo_l.at[ci]))
            else:
                out.append(remote(src, dst, zo_s.at[ci, flip - 1], zo_r.at[ci, flip - 1], flip))
        return out

    def te_chunk(ci, carry):
        q = ci // 2
        hf = ci % 2
        h16 = pl.multiple_of(hf * 16, 16)
        for c2 in range(2):
            for k in range(2):
                for r in range(B):
                    rows = pl.ds(((2 * k + c2) * B + r) * TRI_PITCH, 16)
                    zf[rows] = zx[c2, k * B + r, q, pl.ds(h16, 16), :].astype(F32)

        def te_x(p):
            return jnp.concatenate([zf[pl.ds(2 * p + u, N, stride=TRI_PITCH), :] for u in range(2)], axis=0)

        def te_emit(p, slot, new):
            for u in range(2):
                zof[pl.ds(2 * p + u, N, stride=TRI_PITCH), :] = new[N * u:N * u + N]

        te = Attention(st, w_te, w_te_o, 4, te_x, lambda h: bte[h], lambda p, u: None, te_emit)

        def te_four(t, carry2):
            for e in range(4):
                te.step(4 * t + e, e, 7)
            return carry2
        te.begin()
        lax.fori_loop(0, 2, te_four, 0)
        te.end(7)
        for r in range(N):
            zo[r, q, pl.ds(h16, 16), :] = zof[pl.ds(r * TRI_PITCH, 16), :].astype(BF16)
        for cpy in zo_copies(ci, q, hf):
            cpy.start()
        return carry
    lax.fori_loop(0, 4, te_chunk, 0)

    for cpy in b_copies + bs_copies + be_copies + [z_copy]:
        cpy.wait_send()
    def drain8(j, carry):
        m_chunk(j).wait_send()
        zx_copy(j).wait_send()
        x_chunk(j).wait_send()
        return carry
    lax.fori_loop(0, 8, drain8, 0)
    for q in range(2):
        c_copy(q).wait_send()
        for cpy in mo_copies(q):
            cpy.wait()
    def drain4(ci, carry):
        for cpy in zo_copies(ci, ci // 2, ci % 2):
            cpy.wait()
        return carry
    lax.fori_loop(0, 4, drain4, 0)


def weight_t(w):
    return w.reshape(w.shape[0], -1).T


def solution(mesh):
    rows_spec = P(PART_AXIS, GROUP_AXIS, None, None)
    in_specs = (rows_spec, rows_spec, P(PART_AXIS, None, None), P(PART_AXIS, None)) + (P(),) * 13

    def block(m, z, mask, res_mask, *weights):
        (w_row_bias, w_row_qkvg, w_row_out, w_col_qkvg, w_col_out, w_opm_ac, w_opm_out,
         w_ts_bias, w_ts_qkvg, w_ts_out, w_te_bias, w_te_qkvg, w_te_out) = weights
        dev = lax.axis_index(GROUP_AXIS)
        x = dev // 2
        c = dev % 2
        mbias = (lax.dynamic_index_in_dim(mask, x, 0, False).astype(F32) - 1.0) * (MASK_SCALE * LOG2E)
        mrow = lax.dynamic_index_in_dim(mbias.reshape(2, 2, B, N), c, 1, False)
        mrow = mrow.reshape(B, 2, N).swapaxes(1, 2)
        mcol = lax.dynamic_index_in_dim(mbias.T.reshape(2, 2, B, N), c, 1, False)
        mcol = mcol.reshape(B, 2, N).swapaxes(1, 2)
        mres = (lax.dynamic_index_in_dim(res_mask, x, 0, False).astype(F32) - 1.0) * (MASK_SCALE * LOG2E)
        args = (m, z, mask, mrow, mcol, mres[:, None], w_row_bias.T, w_ts_bias.T, w_te_bias.T,
                weight_t(w_row_qkvg), w_row_out.reshape(W, W), weight_t(w_col_qkvg), w_col_out.reshape(W, W),
                weight_t(w_opm_ac), w_opm_out.reshape(K1, N),
                weight_t(w_ts_qkvg), w_ts_out.reshape(N, N), weight_t(w_te_qkvg), w_te_out.reshape(N, N))
        vm = pl.BlockSpec(memory_space=pltpu.VMEM)
        hbm = pl.BlockSpec(memory_space=pl.ANY)
        V = pltpu.VMEM
        row_z, row_m, sq = (B, N, N), (B, N, W), (N, N)
        scratch = [V(shape, BF16) for shape in (
            (2,) + row_z, row_z, (2,) + row_m, (2, 64, 2, B, W), (64, 2, B, W), (1280, N))]
        scratch += [V(shape, F32) for shape in (
            (K1, N), (8,) + sq) + ((N * COL_PITCH, N),) * 4]
        scratch += [V((N, 2, B, W), BF16), V((2048, N), BF16), V((B * N, N), BF16), V((N * COL_PITCH, N), F32),
                    V((B * N, N), BF16), V(sq, F32), V(sq, F32), V((N, K1), BF16), V((2, 8, K1, N), BF16)]
        scratch += [V(shape, F32) for shape in ((K1, N), (4,) + sq, (K1, N), (4,) + sq)]
        scratch += [V((2, 64, 2, B, N), BF16), V((64, 2, B, N), BF16), V((N * TRI_PITCH, N), F32), V((N * TRI_PITCH, N), F32),
                    V((N, 2, B, N), BF16)]
        scratch += [V((2, W, W), BF16)] * 2 + [V((4, W, W), BF16), V((4, W, W), F32), V((2, 16) + sq, F32),
                    V((2, 16, N), F32), V((2, W, W), BF16), V((2, W, W), BF16), V((8, N), F32), V((8, N), F32)]
        S = pltpu.SemaphoreType.DMA
        scratch += [S(shape) for shape in (
            (3,), (8,), (8,), (1,), (1,), (3,), (3,), (8,), (8,), (2, 3), (2, 3), (2,), (2,), (2,),
            (2,), (2,), (2,), (2,), (8,), (8,), (4, 3), (4, 3), (4,))]
        return pl.pallas_call(
            mega,
            out_shape=(jax.ShapeDtypeStruct(m.shape, BF16), jax.ShapeDtypeStruct(z.shape, BF16)),
            in_specs=[hbm, hbm] + [vm] * 17,
            out_specs=(hbm, hbm),
            scratch_shapes=scratch,
            compiler_params=pltpu.CompilerParams(collective_id=0, has_side_effects=True,
                                                 vmem_limit_bytes=62 << 20),
            name='evoformer_block',
        )(*args)

    return jax.shard_map(block, mesh=mesh, in_specs=in_specs, out_specs=(rows_spec, rows_spec), check_vma=False)
```

time: 677 us -> 178 us (0.26); the launches traced: 665 us -> 177 us
  matrix products: 254 us -> 0 us
  Pallas kernels: 0 us -> 163 us
  local copies, waits for them, and re-layouts: 153 us -> 11 us
  blocking collectives: 103 us -> 0 us
  other arithmetic: 96.2 us -> 2.4 us
  starting transfers between devices: 32.9 us -> 0 us
  between operations: 15.5 us -> 0.7 us
  waiting for transfers between devices: 11.4 us -> 0 us
    dot_general x36 -> x0, matrix products: 229 us -> none  [the longest x8 71.3 us: gated_attention(): jnp.einsum('qhd,hdc->qc', mixed.astype(jnp.bfloat16), w_out, preferred_el...]
    pallas_call x0 -> x1, Pallas kernels: none -> 163 us  [block(): pl.pallas_call(mega, out_shape=(jax.ShapeDtypeStruct(m.shape, BF16), jax....]
    dot_general x2 -> x0, local copies, waits for them, and re-layouts: 104 us -> none  [one_row(): jnp.einsum('se,jsf->jef', left_row, right_proj, preferred_element_type=jn...]
    all_gather x6 -> x0, blocking collectives: 103 us -> none  [gathered_bias(): return lax.all_gather(bias_part, GROUP_AXIS, axis=1, tiled=True)]
    sub x6 -> x0, other arithmetic: 61.7 us -> none  [gated_attention(): attn_prob = jax.nn.softmax(logits, axis=-1).astype(jnp.bfloat16)]
    all_to_all x8 -> x0, starting transfers between devices: 32.2 us -> none  [the longest x2 9.1 us: crop_block(): lax.all_to_all(value_a8, GROUP_AXIS, 1, 0, tiled=True)]
    convert_element_type x20 -> x0, local copies, waits for them, and re-layouts: 27.8 us -> none  [the longest x12 26.8 us: gated_attention(): return (x_row.astype(jnp.float32) + update).astype(jnp.bfloat16)]
    sub x2 -> x0, matrix products: 24.7 us -> none  [gated_attention(): attn_prob = jax.nn.softmax(logits, axis=-1).astype(jnp.bfloat16)]
  transfers between devices with their start and end apart: 10 -> 0, of which waited for: 2 -> 0; matrix products, arithmetic and copies ran while one was open for 50% -> 0% of each run, Pallas kernels for 0% -> 0%
where the time goes in v1:
time: 178 us; the launch traced here: 177 us
  Pallas kernels  163 us (92%)
  local copies, waits for them, and re-layouts  11 us (6%)
  other arithmetic  2.4 us (1%)
    pallas_call x1, Pallas kernels, block(): pl.pallas_call(mega, out_shape=(jax.ShapeDtypeStruct(m.shape, BF16), jax....  163 us
    unnamed x4, local copies, waits for them, and re-layouts  6.17 us

profile of v1, /device:TPU:0, one launch (start us, length us, event | category | flops | bytes accessed | tf_op | source)
XLA Modules:
  0.0 177.3 jit_solution(7258168883464480118)
XLA Ops:
  0.7 0.7 fusion.3
  1.3 0.7 copy.27.mres_ref
  2.1 0.8 fusion.4
  2.9 0.1 copy.25
  3.0 0.9 add_multiply_fusion
  3.9 2.0 %copy.24 = f32[32,2,128]{1,2,0:T(8,128)} copy(f32[32,2,128]{2,1,0:T(2,128)S(1)} %bitcast.47) | data formatting | bytes 65536 | tf_op jit(solution)/shard_map/reshape | solution.py:543
  5.9 2.0 %copy.26 = f32[32,2,128]{1,2,0:T(8,128)} copy(f32[32,2,128]{2,1,0:T(2,128)S(1)} %bitcast.46) | data formatting | bytes 65536 | tf_op jit(solution)/shard_map/reshape | solution.py:545
  7.9 163.3 %evoformer_block.1 = (bf16[2,32,128,256]{3,2,1,0:T(8,128)(2,1)}, bf16[2,32,128,128]{3,2,1,0:T(8,128)(2,1)}) custom-call(bf16[2,32,128,256]{3,2,1,0:T(8,128)(2,1)} %m_in.1, bf16[2,32,128,128]{3,2,1,0:T(8,128)(2,1)} %z_in.1, s32[2,128,128]{2,1,0:T(8,128)} %mask_ref.1, f32[32,128,2]{2,1,0:T(8,128)} %bitcast.35, f32[32,128,2]{2,1,0:T(8,128)} %bitcast.36, ...), custom_call_target="tpu_custom_call" | custom-call | tf_op jit(solution)/shard_map/evoformer_block/pallas_call | solution.py:570
  171.2 0.0 copy-start
  171.2 4.8 %copy.30 = bf16[2,32,128,256]{3,2,1,0:T(8,128)(2,1)} copy(bf16[2,32,128,256]{3,2,1,0:T(8,128)(2,1)} %get-tuple-element.6) | data formatting | bytes 8388608
  176.0 0.0 copy-done
  176.0 1.3 copy.31
  (1 shorter events, 0.0 us)
Async XLA Ops:
  171.2 4.9 %copy-start = (bf16[2,32,128,128]{3,2,1,0:T(8,128)(2,1)S(1)}, bf16[2,32,128,128]{3,2,1,0:T(8,128)(2,1)}, u32[]{:S(2)}) copy-start(bf16[2,32,128,128]{3,2,1,0:T(8,128)(2,1)} %get-tuple-element.7) | copy-start | bytes 6291460

commit v2 on v1

--- a/solution.py
+++ b/solution.py
@@ -138,10 +138,10 @@
     return jnp.concatenate([b[:, :N], b[:, N:]], axis=0)
 
 
-def mega(m_in, z_in, mask_ref, mrow_ref, mcol_ref, mres_ref, w_rb, w_tsb, w_teb, w_row, w_row_o, w_col, w_col_o, w_ac, w_oo,
+def mega(m_in, z_in, mask_ref, res_ref, w_rb, w_tsb, w_teb, w_row, w_row_o, w_col, w_col_o, w_ac, w_oo,
          w_ts, w_ts_o, w_te, w_te_o, m_out, z_out,
          zr, zot, ms, xx, rs, bb, bbf, bt, xf0, xf1, of0, of1, mo, at, ctx, ctf, cp, ninv, mtr, woot, rr,
-         bs, bts, be, bte, zx, zs, zf, zof, zo, qs, ks, vs, gs, lgs, mxs, ots, nw, wtsb, wteb,
+         bs, bts, be, bte, zx, zs, zf, zof, zo, qs, ks, vs, gs, lgs, mxs, ots, nw, wtsb, wteb, mcb, mrb, mrs, mrow, mcol, ut,
          l_sem, mi_s, mi_r, zi_s, zi_r, b_s, b_r, x_s, x_r, mo_s, mo_r, mo_l, c_s, c_r, bs_s, bs_r, be_s, be_r,
          zx_s, zx_r, zo_s, zo_r, zo_l):
     st = (qs, ks, vs, gs, lgs, mxs, ots)
@@ -212,6 +212,16 @@
     mkb = mk.astype(BF16)
     ninv[...] = 1.0 / (mm(mkb, mkb, TN) + OPM_EPS)
     mtr[...] = jnp.transpose(mk)
+    mcb[...] = (mk - 1.0) * (MASK_SCALE * LOG2E)
+    mrb[...] = jnp.transpose(mcb[...])
+    res_bias = (res_ref[pl.ds(x, 1), :].astype(F32) - 1.0) * (MASK_SCALE * LOG2E)
+    mrs[...] = jnp.transpose(jnp.broadcast_to(res_bias, (N, N)))
+    def mask_tables(p, carry):
+        slot = jnp.where(p < 16, x, ox)
+        mrow[p] = pltpu.roll(mrb[...], (N - (2 * slot + c) * B - 2 * (p % 16)) % N, 1)
+        mcol[p] = pltpu.roll(mcb[...], (N - (2 * (p // 16) + c) * B - 2 * (p % 16)) % N, 1)
+        return carry
+    lax.fori_loop(0, B, mask_tables, 0)
     for e in range(B):
         ctf[pl.ds(e * COL_PITCH, B)] = w_oo[B * e:B * e + B].astype(F32)
     def perm_oo(f, carry):
@@ -241,8 +251,8 @@
         s = row_seq(p)
         return ms[s // B, pl.ds(s % B, 2)].reshape(W, W).astype(F32)
 
-    def lane_mask(ref, row, u):
-        return jnp.broadcast_to(ref[row][:, u:u + 1], (N, N))
+    def lane_mask(ref, p, u):
+        return jnp.broadcast_to(ref[p][:, u:u + 1], (N, N))
 
     def row_emit(p, slot, new):
         s = row_seq(p)
@@ -252,7 +262,7 @@
         rs[pl.ds(s, 2)] = jnp.where(c == 0, odd, even).astype(BF16)
 
     row = Attention(st, w_row, w_row_o, 8, row_x, lambda h: bt[h],
-                    lambda p, u: lane_mask(mrow_ref, row_seq(p) // 2, u), row_emit)
+                    lambda p, u: lane_mask(mrow, p, u), row_emit)
 
     def row_four(t, carry):
         @pl.when(jnp.logical_and(t >= 3, t < 7))
@@ -323,7 +333,7 @@
                 of1[pl.ds(2 * p + u, N, stride=COL_PITCH), :] = new[N * u:N * u + N, N:]
 
         col = Attention(st, w_col, w_col_o, 8, col_x, lambda h: None,
-                        lambda p, u: lane_mask(mcol_ref, q * 16 + p, u), col_emit, col_post)
+                        lambda p, u: lane_mask(mcol, q * 16 + p, u), col_emit, col_post)
 
         def col_four(t, carry2):
             for e in range(4):
@@ -365,37 +375,41 @@
                 blk = o[B * i:B * i + B, N * ff:N * ff + N] * nrow
                 rr[slot, i, fp * 64 + B * ff:fp * 64 + B * ff + B] = blk.astype(BF16)
 
-    def opm_load(ib, ip):
-        k, r0, _ = opm_place(ib)
-        return zr[k, pl.ds(r0 + 2 * ip, 2)].reshape(W, N).astype(F32)
-
-    def opm_update(z_old, slot, ip):
-        upd_t = mm(woot[...], jnp.concatenate([rr[slot, 2 * ip], rr[slot, 2 * ip + 1]], axis=1), NN)
-        zn = (z_old + jnp.concatenate([jnp.transpose(upd_t[:, :N]), jnp.transpose(upd_t[:, N:])], axis=0)).astype(BF16)
-        b = side_by_side(mm(wtsb[...].astype(BF16), layer_norm(zn.astype(F32)), NT)).astype(BF16).astype(F32)
-        return zn, b
-
-    def opm_store(ib, ip, zn, b):
-        k, r0, nat0 = opm_place(ib)
-        zr[k, pl.ds(r0 + 2 * ip, 2)] = zn.reshape(2, N, N)
-        bs[rows_at((nat0 + 2 * ip) * 8, 16)] = b
+    def pair_place(p):
+        return p // 16, 2 * (p % 16)
+
+    def opm_product(slot, ip, us):
+        ut[us] = mm(woot[...], jnp.concatenate([rr[slot, 2 * ip], rr[slot, 2 * ip + 1]], axis=1), NN)
+
+    def opm_update(p, us):
+        k, r = pair_place(p)
+        upd = jnp.concatenate([jnp.transpose(ut[us, :, :N]), jnp.transpose(ut[us, :, N:])], axis=0)
+        zn = (zr[k, pl.ds(r, 2)].reshape(W, N).astype(F32) + upd).astype(BF16)
+        nw[us, :, 0:N] = zn
+        ms[k, pl.ds(r, 2), :, 0:N] = zn.reshape(2, N, N)
+
+    def opm_bias(p, us):
+        k, r = pair_place(p)
+        b = mm(wtsb[...].astype(BF16), layer_norm(nw[us, :, 0:N].astype(F32)), NT)
+        bs[rows_at(((2 * k + c) * B + r) * 8, 16)] = side_by_side(b).astype(BF16).astype(F32)
 
     def opm_two(t, carry):
-        for e in range(2):
-            ib = 2 * t + e
-            nxt = jnp.minimum(ib + 1, 7)
-            olds = [opm_load(ib, ip) for ip in range(4)]
-            news = []
-            for ip in range(4):
-                for fp in range(4):
-                    opm_outer(nxt, 1 - e, ip * 4 + fp)
-                news.append(opm_update(olds[ip], e, ip))
-            for ip in range(4):
-                opm_store(ib, ip, *news[ip])
+        for e in range(8):
+            p = 8 * t + e
+            slot = e // 4
+            opm_bias(jnp.maximum(p - 2, 0), e % 2)
+            opm_update(jnp.maximum(p - 1, 0), 1 - e % 2)
+            nxt = jnp.minimum(2 * t + slot + 1, 7)
+            for f in range(4):
+                opm_outer(nxt, 1 - slot, e % 4 * 4 + f)
+            opm_product(slot, e % 4, e % 2)
         return carry
     for fp in range(16):
         opm_outer(0, 0, fp)
     lax.fori_loop(0, 4, opm_two, 0)
+    opm_update(31, 1)
+    opm_bias(30, 0)
+    opm_bias(31, 1)
 
     def tri_bias_copies(ref, s_sem, r_sem):
         out = []
@@ -408,7 +422,7 @@
         cpy.start()
     for cpy in bs_copies:
         cpy.wait_recv()
-    mres = jnp.broadcast_to(mres_ref[...], (N, N))
+    mres = mrs[...]
     for h in range(4):
         bts[h] = jnp.transpose(bs[pl.ds(h, N, stride=8), :]) * LOG2E + mres
 
@@ -417,7 +431,7 @@
         return remote(zs.at[rows], zx.at[c, rows], zx_s.at[ob], zx_r.at[ob], 1)
 
     def ts_x(p):
-        return zr[p // 16, pl.ds(2 * (p % 16), 2)].reshape(W, N).astype(F32)
+        return ms[p // 16, pl.ds(2 * (p % 16), 2), :, 0:N].reshape(W, N).astype(F32)
 
     def ts_post(p, slot):
         b = mm(wteb[...].astype(BF16), layer_norm(nw[slot, :, 0:N].astype(F32)), NT)
@@ -535,16 +549,7 @@
     def block(m, z, mask, res_mask, *weights):
         (w_row_bias, w_row_qkvg, w_row_out, w_col_qkvg, w_col_out, w_opm_ac, w_opm_out,
          w_ts_bias, w_ts_qkvg, w_ts_out, w_te_bias, w_te_qkvg, w_te_out) = weights
-        dev = lax.axis_index(GROUP_AXIS)
-        x = dev // 2
-        c = dev % 2
-        mbias = (lax.dynamic_index_in_dim(mask, x, 0, False).astype(F32) - 1.0) * (MASK_SCALE * LOG2E)
-        mrow = lax.dynamic_index_in_dim(mbias.reshape(2, 2, B, N), c, 1, False)
-        mrow = mrow.reshape(B, 2, N).swapaxes(1, 2)
-        mcol = lax.dynamic_index_in_dim(mbias.T.reshape(2, 2, B, N), c, 1, False)
-        mcol = mcol.reshape(B, 2, N).swapaxes(1, 2)
-        mres = (lax.dynamic_index_in_dim(res_mask, x, 0, False).astype(F32) - 1.0) * (MASK_SCALE * LOG2E)
-        args = (m, z, mask, mrow, mcol, mres[:, None], w_row_bias.T, w_ts_bias.T, w_te_bias.T,
+        args = (m, z, mask, res_mask, w_row_bias.T, w_ts_bias.T, w_te_bias.T,
                 weight_t(w_row_qkvg), w_row_out.reshape(W, W), weight_t(w_col_qkvg), w_col_out.reshape(W, W),
                 weight_t(w_opm_ac), w_opm_out.reshape(K1, N),
                 weight_t(w_ts_qkvg), w_ts_out.reshape(N, N), weight_t(w_te_qkvg), w_te_out.reshape(N, N))
@@ -563,6 +568,7 @@
                     V((N, 2, B, N), BF16)]
         scratch += [V((2, W, W), BF16)] * 2 + [V((4, W, W), BF16), V((4, W, W), F32), V((2, 16) + sq, F32),
                     V((2, 16, N), F32), V((2, W, W), BF16), V((2, W, W), BF16), V((8, N), F32), V((8, N), F32)]
+        scratch += [V(sq, F32)] * 3 + [V((B,) + sq, F32)] * 2 + [V((2, N, W), F32)]
         S = pltpu.SemaphoreType.DMA
         scratch += [S(shape) for shape in (
             (3,), (8,), (8,), (1,), (1,), (3,), (3,), (8,), (8,), (2, 3), (2, 3), (2,), (2,), (2,),
@@ -570,7 +576,7 @@
         return pl.pallas_call(
             mega,
             out_shape=(jax.ShapeDtypeStruct(m.shape, BF16), jax.ShapeDtypeStruct(z.shape, BF16)),
-            in_specs=[hbm, hbm] + [vm] * 17,
+            in_specs=[hbm, hbm] + [vm] * 15,
             out_specs=(hbm, hbm),
             scratch_shapes=scratch,
             compiler_params=pltpu.CompilerParams(collective_id=0, has_side_effects=True,

time: 178 us -> 161 us (0.904)
  Pallas kernels: 163 us -> 154 us
  local copies, waits for them, and re-layouts: 11 us -> 6.17 us
  other arithmetic: 2.4 us -> 0 us
    pallas_call x1, Pallas kernels: 163 us -> 154 us  [block(): pl.pallas_call(mega, out_shape=(jax.ShapeDtypeStruct(m.shape, BF16), jax....]
    reshape x2 -> x0, local copies, waits for them, and re-layouts: 3.95 us -> none  [the longest x1 1.98 us: block(): mrow = mrow.reshape(B, 2, N).swapaxes(1, 2)]
where the time goes in v2:
time: 161 us
  Pallas kernels  154 us (96%)
  local copies, waits for them, and re-layouts  6.17 us (4%)
    pallas_call x1, Pallas kernels, block(): pl.pallas_call(mega, out_shape=(jax.ShapeDtypeStruct(m.shape, BF16), jax....  154 us
    unnamed x4, local copies, waits for them, and re-layouts  6.17 us

profile of v2, /device:TPU:0, one launch (start us, length us, event | category | flops | bytes accessed | tf_op | source)
XLA Modules:
  0.0 161.1 jit_solution(13522725909092261559)
XLA Ops:
  0.6 154.3 %evoformer_block.1 = (bf16[2,32,128,256]{3,2,1,0:T(8,128)(2,1)}, bf16[2,32,128,128]{3,2,1,0:T(8,128)(2,1)}) custom-call(bf16[2,32,128,256]{3,2,1,0:T(8,128)(2,1)} %m_in.1, bf16[2,32,128,128]{3,2,1,0:T(8,128)(2,1)} %z_in.1, s32[2,128,128]{2,1,0:T(8,128)} %mask_ref.1, s32[2,128]{1,0:T(2,128)} %res_ref.1, bf16[8,128]{1,0:T(8,128)(2,1)} %bitcast.33, ...), custom_call_target="tpu_custom_call" | custom-call | tf_op jit(solution)/shard_map/evoformer_block/pallas_call | solution.py:576
  154.9 0.0 copy-start
  154.9 4.8 %copy.21 = bf16[2,32,128,256]{3,2,1,0:T(8,128)(2,1)} copy(bf16[2,32,128,256]{3,2,1,0:T(8,128)(2,1)} %get-tuple-element.4) | data formatting | bytes 8388608
  159.8 0.0 copy-done
  159.8 1.3 copy.22
Async XLA Ops:
  154.9 4.9 %copy-start = (bf16[2,32,128,128]{3,2,1,0:T(8,128)(2,1)S(1)}, bf16[2,32,128,128]{3,2,1,0:T(8,128)(2,1)}, u32[]{:S(2)}) copy-start(bf16[2,32,128,128]{3,2,1,0:T(8,128)(2,1)} %get-tuple-element.5) | copy-start | bytes 6291460

commit v3 on v2

--- a/solution.py
+++ b/solution.py
@@ -18,6 +18,7 @@
 B = 32
 W = 256
 K1 = 1024
+T16 = 16
 COL_PITCH = 40
 TRI_PITCH = 24
 SCALE2 = (HEAD_DIM ** -0.5) * LOG2E
@@ -140,9 +141,9 @@
 
 def mega(m_in, z_in, mask_ref, res_ref, w_rb, w_tsb, w_teb, w_row, w_row_o, w_col, w_col_o, w_ac, w_oo,
          w_ts, w_ts_o, w_te, w_te_o, m_out, z_out,
-         zr, zot, ms, xx, rs, bb, bbf, bt, xf0, xf1, of0, of1, mo, at, ctx, ctf, cp, ninv, mtr, woot, rr,
+         zr, zot, ms, xx, rst, bbx, bbo, bbf, bt, xf0, xf1, of0, of1, mo, at, ctx, ctf, cp, ninv, mtr, woot, rr,
          bs, bts, be, bte, zx, zs, zf, zof, zo, qs, ks, vs, gs, lgs, mxs, ots, nw, wtsb, wteb, mcb, mrb, mrs, mrow, mcol, ut,
-         l_sem, mi_s, mi_r, zi_s, zi_r, b_s, b_r, x_s, x_r, mo_s, mo_r, mo_l, c_s, c_r, bs_s, bs_r, be_s, be_r,
+         l_sem, zi_s, zi_r, b_s, b_r, xa_s, xa_r, xb_s, xb_r, mo_s, mo_r, mo_l, c_s, c_r, bs_s, bs_r, be_s, be_r,
          zx_s, zx_r, zo_s, zo_r, zo_l):
     st = (qs, ks, vs, gs, lgs, mxs, ots)
     dat = lax.axis_index(PART_AXIS)
@@ -165,45 +166,40 @@
         pl.semaphore_signal(barrier, inc=1, device_id=(dat, peer(flip)), device_id_type=MESH_ID)
     cp_zo = pltpu.make_async_copy(z_in.at[ox], zot, l_sem.at[0])
     cp_zr = pltpu.make_async_copy(z_in.at[x], zr.at[x], l_sem.at[1])
-    cp_m = pltpu.make_async_copy(m_in.at[x], ms.at[x], l_sem.at[2])
-    cp_zo.start()
-    cp_zr.start()
-    cp_m.start()
+    cp_mo = pltpu.make_async_copy(m_in.at[ox], ms.at[ox], l_sem.at[2])
+    cp_mx = pltpu.make_async_copy(m_in.at[x], ms.at[x], l_sem.at[3])
+    for cpy in (cp_zr, cp_zo, cp_mo, cp_mx):
+        cpy.start()
     pl.semaphore_wait(barrier, 3)
 
-    def m_chunk(j):
-        return remote(m_in.at[ox, pl.ds(4 * j, 4)], ms.at[x, pl.ds(4 * j, 4)], mi_s.at[j], mi_r.at[j], 2)
-
-    m_chunk(0).start()
-
-    def bias_rows(load, base):
+    z_copies = []
+    for n, (first, size) in enumerate(((0, 4), (4, 8), (12, 20))):
+        rows = pl.ds(first, size)
+        z_copies.append(remote(z_in.at[ox, rows], zr.at[x, rows], zi_s.at[n], zi_r.at[n], 2))
+    z_copies[0].start()
+
+    row0 = pl.multiple_of(dev * W, W)
+    own = pl.ds(row0, W)
+
+    def bias_rows(load, dst):
         def body(g, carry):
             for p in range(4):
                 y = layer_norm(load(8 * g + 2 * p).reshape(W, N).astype(F32))
-                b = side_by_side(mm(w_rb[...], y, NT)).astype(BF16)
-                bb[rows_at(base + 64 * g + 16 * p, 16)] = b
+                dst[rows_at(row0 + 64 * g + T16 * p, T16)] = side_by_side(mm(w_rb[...], y, NT)).astype(BF16)
             return carry
         lax.fori_loop(0, 4, body, 0)
 
-    row0 = pl.multiple_of(dev * W, W)
-    spare = K1
+    b_copies = [remote(src.at[own], dst.at[own], b_s.at[n], b_r.at[n], flip) for n, (src, dst, flip) in enumerate((
+        (bbx, bbo, 2), (bbx, bbo, 3), (bbo, bbo, 1), (bbo, bbx, 2), (bbo, bbx, 3), (bbx, bbx, 1)))]
+    cp_zr.wait()
+    bias_rows(lambda r: zr[x, pl.ds(r, 2)], bbx)
+    for cpy in b_copies[:2]:
+        cpy.start()
     cp_zo.wait()
-    bias_rows(lambda r: zot[pl.ds(r, 2)], spare)
-    b_copies = []
-    for n, flip in enumerate((2, 3)):
-        b_copies.append(remote(bb.at[pl.ds(spare, W)], bb.at[pl.ds(row0, W)], b_s.at[n], b_r.at[n], flip))
-    for cpy in b_copies:
+    bias_rows(lambda r: zot[pl.ds(r, 2)], bbo)
+    for cpy in b_copies[2:]:
         cpy.start()
-    for j in range(1, 8):
-        m_chunk(j).start()
-    z_copy = remote(z_in.at[ox], zr.at[x], zi_s.at[0], zi_r.at[0], 2)
-    z_copy.start()
-    cp_zr.wait()
-
-    bias_rows(lambda r: zr[x, pl.ds(r, 2)], row0)
-    b_own = remote(bb.at[pl.ds(row0, W)], bb.at[pl.ds(row0, W)], b_s.at[2], b_r.at[2], 1)
-    b_own.start()
-    b_copies.append(b_own)
+    z_copies[1].start()
 
     for wdst, wsrc in ((wtsb, w_tsb), (wteb, w_teb)):
         wdst[0:4] = wsrc[...].astype(F32)
@@ -213,13 +209,13 @@
     ninv[...] = 1.0 / (mm(mkb, mkb, TN) + OPM_EPS)
     mtr[...] = jnp.transpose(mk)
     mcb[...] = (mk - 1.0) * (MASK_SCALE * LOG2E)
-    mrb[...] = jnp.transpose(mcb[...])
+    mrb[1] = jnp.transpose(mcb[...])
+    mrb[0] = jnp.transpose((mask_ref[ox].astype(F32) - 1.0) * (MASK_SCALE * LOG2E))
     res_bias = (res_ref[pl.ds(x, 1), :].astype(F32) - 1.0) * (MASK_SCALE * LOG2E)
     mrs[...] = jnp.transpose(jnp.broadcast_to(res_bias, (N, N)))
     def mask_tables(p, carry):
-        slot = jnp.where(p < 16, x, ox)
-        mrow[p] = pltpu.roll(mrb[...], (N - (2 * slot + c) * B - 2 * (p % 16)) % N, 1)
-        mcol[p] = pltpu.roll(mcb[...], (N - (2 * (p // 16) + c) * B - 2 * (p % 16)) % N, 1)
+        mrow[p] = pltpu.roll(mrb[p // T16], (N - dev * B - 2 * (p % T16)) % N, 1)
+        mcol[p] = pltpu.roll(mcb[...], (N - (2 * (p // T16) + c) * B - 2 * (p % T16)) % N, 1)
         return carry
     lax.fori_loop(0, B, mask_tables, 0)
     for e in range(B):
@@ -231,61 +227,72 @@
     for t in range(8):
         woot[:, N * t:N * t + N] = jnp.transpose(xf0[N * t:N * t + N, :]).astype(BF16)
 
-    for cpy in b_copies:
-        cpy.wait_recv()
-    bbf[...] = bb[0:K1].astype(F32) * LOG2E
-    for h in range(8):
-        bt[h] = jnp.transpose(bbf[pl.ds(h, N, stride=8), :])
-
-    cp_m.wait()
-
-    def x_chunk(ch):
-        k = jnp.where(ch < 4, x, ox)
-        rows = rows_at(k * B + (ch % 4) * 8, 8)
-        return remote(rs.at[rows], xx.at[c, rows], x_s.at[ch], x_r.at[ch], 1)
-
-    def row_seq(p):
-        return jnp.where(p < 16, x, ox) * B + 2 * (p % 16)
+    def bias_table(n, src):
+        for cpy in b_copies[3 * n:3 * n + 3]:
+            cpy.wait_recv()
+        bbf[...] = src[...].astype(F32) * LOG2E
+        for h in range(8):
+            bt[n, h] = jnp.transpose(bbf[pl.ds(h, N, stride=8), :])
+    bias_table(0, bbo)
+
+    cp_mo.wait()
+    cp_mx.wait()
+
+    def xa_copy(q, t, rel):
+        rows = rows_at(t * 8, 8)
+        return remote(rst.at[rel, rows, q], xx.at[1 + rel, rows, q], xa_s.at[q, t, rel], xa_r.at[q, t, rel], 2 + rel)
+
+    def xb_copy(t):
+        return remote(rst.at[1, rows_at(B + t * 8, 8)], xx.at[0, rows_at(t * 8, 8)], xb_s.at[t], xb_r.at[t], 1)
 
     def row_x(p):
-        s = row_seq(p)
-        return ms[s // B, pl.ds(s % B, 2)].reshape(W, W).astype(F32)
+        return ms[jnp.where(p < T16, ox, x), pl.ds(2 * (p % T16), 2)].reshape(W, W).astype(F32)
 
     def lane_mask(ref, p, u):
         return jnp.broadcast_to(ref[p][:, u:u + 1], (N, N))
 
     def row_emit(p, slot, new):
-        s = row_seq(p)
         new = new.reshape(2, 2, 2, B, W)
         even, odd = new[:, :, 0], new[:, :, 1]
-        xx[c, pl.ds(s, 2)] = jnp.where(c == 0, even, odd).astype(BF16)
-        rs[pl.ds(s, 2)] = jnp.where(c == 0, odd, even).astype(BF16)
-
-    row = Attention(st, w_row, w_row_o, 8, row_x, lambda h: bt[h],
-                    lambda p, u: lane_mask(mrow, p, u), row_emit)
+        rst[0, pl.ds(2 * p, 2)] = jnp.where(c == 0, even, odd).astype(BF16)
+        rst[1, pl.ds(2 * p, 2)] = jnp.where(c == 0, odd, even).astype(BF16)
 
     def row_four(t, carry):
-        @pl.when(jnp.logical_and(t >= 3, t < 7))
+        @pl.when(t == 3)
         def _():
-            m_chunk(2 * t - 6).wait_recv()
-            m_chunk(2 * t - 5).wait_recv()
+            bias_table(1, bbx)
+
+        def bias_at(p):
+            return lambda h: bt[jnp.minimum(p + 1, 31) // T16, h]
 
         for e in range(4):
+            row = Attention(st, w_row, w_row_o, 8, row_x, bias_at(4 * t + e),
+                            lambda p, u: lane_mask(mrow, p, u), row_emit)
             row.step(4 * t + e, e, 31)
 
-        @pl.when(t > 0)
+        @pl.when(jnp.logical_and(t > 0, t < 5))
         def _():
-            x_chunk(t - 1).start()
-        return carry
+            for rel in range(2):
+                xa_copy(0, t - 1, rel).start()
+
+        @pl.when(t == 4)
+        def _():
+            for tt in range(4):
+                for rel in range(2):
+                    xa_copy(1, tt, rel).start()
+            z_copies[2].start()
+
+        @pl.when(t > 4)
+        def _():
+            xb_copy(t - 5).start()
+        return carry
+    row = Attention(st, w_row, w_row_o, 8, row_x, lambda h: bt[0, h], lambda p, u: lane_mask(mrow, p, u), row_emit)
     row.begin()
     lax.fori_loop(0, 8, row_four, 0)
     row.end(31)
-    x_chunk(7).start()
-
-    def x_wait(ch, carry):
-        x_chunk(ch).wait_recv()
-        return carry
-    lax.fori_loop(0, 8, x_wait, 0)
+    xb_copy(3).start()
+    for t in range(4):
+        xb_copy(t).wait_recv()
 
     def mo_copies(q):
         out = []
@@ -309,13 +316,16 @@
             for u in range(2)], axis=0)
 
     def col_chunk(q, carry):
-        for c2 in range(2):
-            for k in range(2):
-                for r in range(B):
-                    v = xx[c2, k * B + r, q].astype(F32)
-                    rows = pl.ds(((2 * k + c2) * B + r) * COL_PITCH, B)
-                    xf0[rows] = v[:, :N]
-                    xf1[rows] = v[:, N:]
+        for t in range(4):
+            for rel in range(2):
+                xa_copy(q, t, rel).wait_recv()
+        for flip in range(4):
+            base = peer(flip) * (B * COL_PITCH)
+            for r in range(B):
+                v = (xx[flip - 1, r, q] if flip else rst[0, B + r, q]).astype(F32)
+                rows = pl.ds(pl.multiple_of(base + r * COL_PITCH, 8), B)
+                xf0[rows] = v[:, :N]
+                xf1[rows] = v[:, N:]
 
         def col_post(p, slot):
             ac = mm(w_ac[...], layer_norm(nw[slot].astype(F32)), NT).astype(BF16).astype(F32)
@@ -333,7 +343,7 @@
                 of1[pl.ds(2 * p + u, N, stride=COL_PITCH), :] = new[N * u:N * u + N, N:]
 
         col = Attention(st, w_col, w_col_o, 8, col_x, lambda h: None,
-                        lambda p, u: lane_mask(mcol, q * 16 + p, u), col_emit, col_post)
+                        lambda p, u: lane_mask(mcol, q * T16 + p, u), col_emit, col_post)
 
         def col_four(t, carry2):
             for e in range(4):
@@ -360,7 +370,8 @@
         cp[rows_at(f * N, N)] = ctf[pl.ds(f, N, stride=COL_PITCH), :].astype(BF16)
         return carry
     lax.fori_loop(0, B, perm_c, 0)
-    z_copy.wait_recv()
+    for cpy in z_copies:
+        cpy.wait_recv()
 
     def opm_place(ib):
         k, r0 = ib // 4, (ib % 4) * 8
@@ -376,7 +387,7 @@
                 rr[slot, i, fp * 64 + B * ff:fp * 64 + B * ff + B] = blk.astype(BF16)
 
     def pair_place(p):
-        return p // 16, 2 * (p % 16)
+        return p // T16, 2 * (p % T16)
 
     def opm_product(slot, ip, us):
         ut[us] = mm(woot[...], jnp.concatenate([rr[slot, 2 * ip], rr[slot, 2 * ip + 1]], axis=1), NN)
@@ -391,7 +402,7 @@
     def opm_bias(p, us):
         k, r = pair_place(p)
         b = mm(wtsb[...].astype(BF16), layer_norm(nw[us, :, 0:N].astype(F32)), NT)
-        bs[rows_at(((2 * k + c) * B + r) * 8, 16)] = side_by_side(b).astype(BF16).astype(F32)
+        bs[rows_at(((2 * k + c) * B + r) * 8, T16)] = side_by_side(b).astype(BF16).astype(F32)
 
     def opm_two(t, carry):
         for e in range(8):
@@ -404,7 +415,7 @@
                 opm_outer(nxt, 1 - slot, e % 4 * 4 + f)
             opm_product(slot, e % 4, e % 2)
         return carry
-    for fp in range(16):
+    for fp in range(T16):
         opm_outer(0, 0, fp)
     lax.fori_loop(0, 4, opm_two, 0)
     opm_update(31, 1)
@@ -431,12 +442,12 @@
         return remote(zs.at[rows], zx.at[c, rows], zx_s.at[ob], zx_r.at[ob], 1)
 
     def ts_x(p):
-        return ms[p // 16, pl.ds(2 * (p % 16), 2), :, 0:N].reshape(W, N).astype(F32)
+        return ms[p // T16, pl.ds(2 * (p % T16), 2), :, 0:N].reshape(W, N).astype(F32)
 
     def ts_post(p, slot):
         b = mm(wteb[...].astype(BF16), layer_norm(nw[slot, :, 0:N].astype(F32)), NT)
-        nat = (2 * (p // 16) + c) * B + 2 * (p % 16)
-        be[rows_at(nat * 8, 16)] = side_by_side(b).astype(BF16).astype(F32)
+        nat = (2 * (p // T16) + c) * B + 2 * (p % T16)
+        be[rows_at(nat * 8, T16)] = side_by_side(b).astype(BF16).astype(F32)
 
     def ts_emit(p, slot, new):
         nw[slot, :, 0:N] = new.astype(BF16)
@@ -474,12 +485,12 @@
 
     def zo_copies(ci, q, hf):
         out = []
-        col0 = pl.multiple_of((2 * q + c) * B + hf * 16, 16)
-        h16 = pl.multiple_of(hf * 16, 16)
+        col0 = pl.multiple_of((2 * q + c) * B + hf * T16, T16)
+        h16 = pl.multiple_of(hf * T16, T16)
         for flip in range(4):
             home = peer(flip)
-            src = zo.at[pl.ds(home * B, B), q, pl.ds(h16, 16)]
-            dst = z_out.at[x, :, pl.ds(col0, 16)]
+            src = zo.at[pl.ds(home * B, B), q, pl.ds(h16, T16)]
+            dst = z_out.at[x, :, pl.ds(col0, T16)]
             if flip == 0:
                 out.append(pltpu.make_async_copy(src, dst, zo_l.at[ci]))
             else:
@@ -489,12 +500,12 @@
     def te_chunk(ci, carry):
         q = ci // 2
         hf = ci % 2
-        h16 = pl.multiple_of(hf * 16, 16)
+        h16 = pl.multiple_of(hf * T16, T16)
         for c2 in range(2):
             for k in range(2):
                 for r in range(B):
-                    rows = pl.ds(((2 * k + c2) * B + r) * TRI_PITCH, 16)
-                    zf[rows] = zx[c2, k * B + r, q, pl.ds(h16, 16), :].astype(F32)
+                    rows = pl.ds(((2 * k + c2) * B + r) * TRI_PITCH, T16)
+                    zf[rows] = zx[c2, k * B + r, q, pl.ds(h16, T16), :].astype(F32)
 
         def te_x(p):
             return jnp.concatenate([zf[pl.ds(2 * p + u, N, stride=TRI_PITCH), :] for u in range(2)], axis=0)
@@ -513,20 +524,23 @@
         lax.fori_loop(0, 2, te_four, 0)
         te.end(7)
         for r in range(N):
-            zo[r, q, pl.ds(h16, 16), :] = zof[pl.ds(r * TRI_PITCH, 16), :].astype(BF16)
+            zo[r, q, pl.ds(h16, T16), :] = zof[pl.ds(r * TRI_PITCH, T16), :].astype(BF16)
         for cpy in zo_copies(ci, q, hf):
             cpy.start()
         return carry
     lax.fori_loop(0, 4, te_chunk, 0)
 
-    for cpy in b_copies + bs_copies + be_copies + [z_copy]:
+    for cpy in b_copies + bs_copies + be_copies + z_copies:
         cpy.wait_send()
     def drain8(j, carry):
-        m_chunk(j).wait_send()
         zx_copy(j).wait_send()
-        x_chunk(j).wait_send()
         return carry
     lax.fori_loop(0, 8, drain8, 0)
+    for t in range(4):
+        xb_copy(t).wait_send()
+        for rel in range(2):
+            xa_copy(0, t, rel).wait_send()
+            xa_copy(1, t, rel).wait_send()
     for q in range(2):
         c_copy(q).wait_send()
         for cpy in mo_copies(q):
@@ -558,20 +572,20 @@
         V = pltpu.VMEM
         row_z, row_m, sq = (B, N, N), (B, N, W), (N, N)
         scratch = [V(shape, BF16) for shape in (
-            (2,) + row_z, row_z, (2,) + row_m, (2, 64, 2, B, W), (64, 2, B, W), (1280, N))]
+            (2,) + row_z, row_z, (2,) + row_m, (3, B, 2, B, W), (2, 64, 2, B, W), (K1, N), (K1, N))]
         scratch += [V(shape, F32) for shape in (
-            (K1, N), (8,) + sq) + ((N * COL_PITCH, N),) * 4]
+            (K1, N), (2, 8) + sq) + ((N * COL_PITCH, N),) * 4]
         scratch += [V((N, 2, B, W), BF16), V((2048, N), BF16), V((B * N, N), BF16), V((N * COL_PITCH, N), F32),
                     V((B * N, N), BF16), V(sq, F32), V(sq, F32), V((N, K1), BF16), V((2, 8, K1, N), BF16)]
         scratch += [V(shape, F32) for shape in ((K1, N), (4,) + sq, (K1, N), (4,) + sq)]
         scratch += [V((2, 64, 2, B, N), BF16), V((64, 2, B, N), BF16), V((N * TRI_PITCH, N), F32), V((N * TRI_PITCH, N), F32),
                     V((N, 2, B, N), BF16)]
-        scratch += [V((2, W, W), BF16)] * 2 + [V((4, W, W), BF16), V((4, W, W), F32), V((2, 16) + sq, F32),
-                    V((2, 16, N), F32), V((2, W, W), BF16), V((2, W, W), BF16), V((8, N), F32), V((8, N), F32)]
-        scratch += [V(sq, F32)] * 3 + [V((B,) + sq, F32)] * 2 + [V((2, N, W), F32)]
+        scratch += [V((2, W, W), BF16)] * 2 + [V((4, W, W), BF16), V((4, W, W), F32), V((2, T16) + sq, F32),
+                    V((2, T16, N), F32), V((2, W, W), BF16), V((2, W, W), BF16), V((8, N), F32), V((8, N), F32)]
+        scratch += [V(sq, F32), V((2,) + sq, F32), V(sq, F32)] + [V((B,) + sq, F32)] * 2 + [V((2, N, W), F32)]
         S = pltpu.SemaphoreType.DMA
         scratch += [S(shape) for shape in (
-            (3,), (8,), (8,), (1,), (1,), (3,), (3,), (8,), (8,), (2, 3), (2, 3), (2,), (2,), (2,),
+            (4,), (3,), (3,), (6,), (6,), (2, 4, 2), (2, 4, 2), (4,), (4,), (2, 3), (2, 3), (2,), (2,), (2,),
             (2,), (2,), (2,), (2,), (8,), (8,), (4, 3), (4, 3), (4,))]
         return pl.pallas_call(
             mega,

time: 161 us -> 156 us (0.969)
  Pallas kernels: 154 us -> 149 us
    pallas_call x1, Pallas kernels: 154 us -> 149 us  [block(): pl.pallas_call(mega, out_shape=(jax.ShapeDtypeStruct(m.shape, BF16), jax....]
where the time goes in v3:
time: 156 us; the launch traced here: 155 us
  Pallas kernels  149 us (96%)
  local copies, waits for them, and re-layouts  6.17 us (4%)
    pallas_call x1, Pallas kernels, block(): pl.pallas_call(mega, out_shape=(jax.ShapeDtypeStruct(m.shape, BF16), jax....  149 us
    unnamed x4, local copies, waits for them, and re-layouts  6.17 us

profile of v3, /device:TPU:0, one launch (start us, length us, event | category | flops | bytes accessed | tf_op | source)
XLA Modules:
  0.0 155.4 jit_solution(4803746624844556428)
XLA Ops:
  0.6 148.6 %evoformer_block.1 = (bf16[2,32,128,256]{3,2,1,0:T(8,128)(2,1)}, bf16[2,32,128,128]{3,2,1,0:T(8,128)(2,1)}) custom-call(bf16[2,32,128,256]{3,2,1,0:T(8,128)(2,1)} %m_in.1, bf16[2,32,128,128]{3,2,1,0:T(8,128)(2,1)} %z_in.1, s32[2,128,128]{2,1,0:T(8,128)} %mask_ref.1, s32[2,128]{1,0:T(2,128)} %res_ref.1, bf16[8,128]{1,0:T(8,128)(2,1)} %bitcast.33, ...), custom_call_target="tpu_custom_call" | custom-call | tf_op jit(solution)/shard_map/evoformer_block/pallas_call | solution.py:590
  149.2 0.0 copy-start
  149.2 4.8 %copy.21 = bf16[2,32,128,256]{3,2,1,0:T(8,128)(2,1)} copy(bf16[2,32,128,256]{3,2,1,0:T(8,128)(2,1)} %get-tuple-element.4) | data formatting | bytes 8388608
  154.1 0.0 copy-done
  154.1 1.3 copy.22
Async XLA Ops:
  149.2 4.9 %copy-start = (bf16[2,32,128,128]{3,2,1,0:T(8,128)(2,1)S(1)}, bf16[2,32,128,128]{3,2,1,0:T(8,128)(2,1)}, u32[]{:S(2)}) copy-start(bf16[2,32,128,128]{3,2,1,0:T(8,128)(2,1)} %get-tuple-element.5) | copy-start | bytes 6291460

commit v4 on v3

--- a/solution.py
+++ b/solution.py
@@ -19,6 +19,7 @@
 W = 256
 K1 = 1024
 T16 = 16
+E8 = 8
 COL_PITCH = 40
 TRI_PITCH = 24
 SCALE2 = (HEAD_DIM ** -0.5) * LOG2E
@@ -43,13 +44,21 @@
 
 class Attention:
     def __init__(self, st, wt_ref, wo_ref, n_heads, load_x, bias_of, mask_of, emit, post=None):
-        self.qs, self.ks, self.vs, self.gs, self.lg, self.mx, self.os = st
+        self.qs, self.ks, self.vs, self.gs, self.lg, self.mx, self.os, self.ys = st
         self.wt, self.wo, self.n_heads, self.hd = wt_ref, wo_ref, n_heads, n_heads * HEAD_DIM
         self.load_x, self.bias_of, self.mask_of, self.emit, self.post = load_x, bias_of, mask_of, emit, post
         self.items = [(u, h) for u in range(2) for h in range(0, n_heads, 2)]
 
-    def p_part(self, y, i, part):
+    def n_parts(self, p, i):
+        xf = self.load_x(p)
+        for b in range(4):
+            rows = slice(64 * b, 64 * b + 64)
+            self.ys[i % 2, rows, 0:xf.shape[1]] = layer_norm(xf[rows])
+            yield
+
+    def p_part(self, i, part):
         hd = self.hd
+        y = self.ys[i % 2, :, 0:self.wt.shape[1]]
         w = self.wt[part * hd:(part + 1) * hd]
         if part == 0:
             self.qs[i % 2, 0:hd] = mm(w, y, NT).astype(BF16)
@@ -107,20 +116,22 @@
         if self.post is not None:
             self.post(jnp.maximum(p - 2, 0), i % 2)
         self.o_part(jnp.maximum(p - 1, 0), i - 1)
-        y = layer_norm(self.load_x(jnp.minimum(p + 2, last)))
+        norm = self.n_parts(jnp.minimum(p + 3, last), i + 3)
         nxt = jnp.minimum(p + 1, last)
         for n, item in enumerate(self.items):
             self.l_part(nxt, i + 1, item)
             self.s_part(i, item)
             for part in range(4):
                 if part * len(self.items) // 4 == n:
-                    self.p_part(y, i + 2, part)
+                    next(norm)
+                    self.p_part(i + 2, part)
 
     def begin(self):
-        for i in range(2):
-            y = layer_norm(self.load_x(i))
-            for part in range(4):
-                self.p_part(y, i, part)
+        for i in range(3):
+            for _ in self.n_parts(i, i):
+                pass
+            for part in range(4 if i < 2 else 0):
+                self.p_part(i, part)
         for item in self.items:
             self.l_part(0, 0, item)
 
@@ -142,10 +153,11 @@
 def mega(m_in, z_in, mask_ref, res_ref, w_rb, w_tsb, w_teb, w_row, w_row_o, w_col, w_col_o, w_ac, w_oo,
          w_ts, w_ts_o, w_te, w_te_o, m_out, z_out,
          zr, zot, ms, xx, rst, bbx, bbo, bbf, bt, xf0, xf1, of0, of1, mo, at, ctx, ctf, cp, ninv, mtr, woot, rr,
-         bs, bts, be, bte, zx, zs, zf, zof, zo, qs, ks, vs, gs, lgs, mxs, ots, nw, wtsb, wteb, mcb, mrb, mrs, mrow, mcol, ut,
+         bs, bts, be, bte, zx, zs, zo, qs, ks, vs, gs, lgs, mxs, ots, ys, nw, wtsb, wteb, mcb, mrb, mrs, mrow, mcol, ut,
          l_sem, zi_s, zi_r, b_s, b_r, xa_s, xa_r, xb_s, xb_r, mo_s, mo_r, mo_l, c_s, c_r, bs_s, bs_r, be_s, be_r,
          zx_s, zx_r, zo_s, zo_r, zo_l):
-    st = (qs, ks, vs, gs, lgs, mxs, ots)
+    st = (qs, ks, vs, gs, lgs, mxs, ots, ys)
+    zf, zof = xf1, of1
     dat = lax.axis_index(PART_AXIS)
     dev = lax.axis_index(GROUP_AXIS)
     x = dev // 2
@@ -173,10 +185,9 @@
     pl.semaphore_wait(barrier, 3)
 
     z_copies = []
-    for n, (first, size) in enumerate(((0, 4), (4, 8), (12, 20))):
+    for n, (first, size) in enumerate(((0, E8), (E8, 24))):
         rows = pl.ds(first, size)
         z_copies.append(remote(z_in.at[ox, rows], zr.at[x, rows], zi_s.at[n], zi_r.at[n], 2))
-    z_copies[0].start()
 
     row0 = pl.multiple_of(dev * W, W)
     own = pl.ds(row0, W)
@@ -184,7 +195,7 @@
     def bias_rows(load, dst):
         def body(g, carry):
             for p in range(4):
-                y = layer_norm(load(8 * g + 2 * p).reshape(W, N).astype(F32))
+                y = layer_norm(load(E8 * g + 2 * p).reshape(W, N).astype(F32))
                 dst[rows_at(row0 + 64 * g + T16 * p, T16)] = side_by_side(mm(w_rb[...], y, NT)).astype(BF16)
             return carry
         lax.fori_loop(0, 4, body, 0)
@@ -199,11 +210,11 @@
     bias_rows(lambda r: zot[pl.ds(r, 2)], bbo)
     for cpy in b_copies[2:]:
         cpy.start()
-    z_copies[1].start()
+    z_copies[0].start()
 
     for wdst, wsrc in ((wtsb, w_tsb), (wteb, w_teb)):
         wdst[0:4] = wsrc[...].astype(F32)
-        wdst[4:8] = jnp.zeros((4, N), F32)
+        wdst[4:E8] = jnp.zeros((4, N), F32)
     mk = mask_ref[x].astype(F32)
     mkb = mk.astype(BF16)
     ninv[...] = 1.0 / (mm(mkb, mkb, TN) + OPM_EPS)
@@ -224,26 +235,26 @@
         xf0[rows_at(B * f, B)] = ctf[pl.ds(f, B, stride=COL_PITCH), :]
         return carry
     lax.fori_loop(0, B, perm_oo, 0)
-    for t in range(8):
+    for t in range(E8):
         woot[:, N * t:N * t + N] = jnp.transpose(xf0[N * t:N * t + N, :]).astype(BF16)
 
     def bias_table(n, src):
         for cpy in b_copies[3 * n:3 * n + 3]:
             cpy.wait_recv()
         bbf[...] = src[...].astype(F32) * LOG2E
-        for h in range(8):
-            bt[n, h] = jnp.transpose(bbf[pl.ds(h, N, stride=8), :])
+        for h in range(E8):
+            bt[n, h] = jnp.transpose(bbf[pl.ds(h, N, stride=E8), :])
     bias_table(0, bbo)
 
     cp_mo.wait()
     cp_mx.wait()
 
     def xa_copy(q, t, rel):
-        rows = rows_at(t * 8, 8)
+        rows = rows_at(t * E8, E8)
         return remote(rst.at[rel, rows, q], xx.at[1 + rel, rows, q], xa_s.at[q, t, rel], xa_r.at[q, t, rel], 2 + rel)
 
     def xb_copy(t):
-        return remote(rst.at[1, rows_at(B + t * 8, 8)], xx.at[0, rows_at(t * 8, 8)], xb_s.at[t], xb_r.at[t], 1)
+        return remote(rst.at[1, rows_at(B + t * E8, E8)], xx.at[0, rows_at(t * E8, E8)], xb_s.at[t], xb_r.at[t], 1)
 
     def row_x(p):
         return ms[jnp.where(p < T16, ox, x), pl.ds(2 * (p % T16), 2)].reshape(W, W).astype(F32)
@@ -266,7 +277,7 @@
             return lambda h: bt[jnp.minimum(p + 1, 31) // T16, h]
 
         for e in range(4):
-            row = Attention(st, w_row, w_row_o, 8, row_x, bias_at(4 * t + e),
+            row = Attention(st, w_row, w_row_o, E8, row_x, bias_at(4 * t + e),
                             lambda p, u: lane_mask(mrow, p, u), row_emit)
             row.step(4 * t + e, e, 31)
 
@@ -280,15 +291,15 @@
             for tt in range(4):
                 for rel in range(2):
                     xa_copy(1, tt, rel).start()
-            z_copies[2].start()
+            z_copies[1].start()
 
         @pl.when(t > 4)
         def _():
             xb_copy(t - 5).start()
         return carry
-    row = Attention(st, w_row, w_row_o, 8, row_x, lambda h: bt[0, h], lambda p, u: lane_mask(mrow, p, u), row_emit)
+    row = Attention(st, w_row, w_row_o, E8, row_x, lambda h: bt[0, h], lambda p, u: lane_mask(mrow, p, u), row_emit)
     row.begin()
-    lax.fori_loop(0, 8, row_four, 0)
+    lax.fori_loop(0, E8, row_four, 0)
     row.end(31)
     xb_copy(3).start()
     for t in range(4):
@@ -323,7 +334,7 @@
             base = peer(flip) * (B * COL_PITCH)
             for r in range(B):
                 v = (xx[flip - 1, r, q] if flip else rst[0, B + r, q]).astype(F32)
-                rows = pl.ds(pl.multiple_of(base + r * COL_PITCH, 8), B)
+                rows = pl.ds(pl.multiple_of(base + r * COL_PITCH, E8), B)
                 xf0[rows] = v[:, :N]
                 xf1[rows] = v[:, N:]
 
@@ -342,7 +353,7 @@
                 of0[pl.ds(2 * p + u, N, stride=COL_PITCH), :] = new[N * u:N * u + N, :N]
                 of1[pl.ds(2 * p + u, N, stride=COL_PITCH), :] = new[N * u:N * u + N, N:]
 
-        col = Attention(st, w_col, w_col_o, 8, col_x, lambda h: None,
+        col = Attention(st, w_col, w_col_o, E8, col_x, lambda h: None,
                         lambda p, u: lane_mask(mcol, q * T16 + p, u), col_emit, col_post)
 
         def col_four(t, carry2):
@@ -374,13 +385,13 @@
         cpy.wait_recv()
 
     def opm_place(ib):
-        k, r0 = ib // 4, (ib % 4) * 8
+        k, r0 = ib // 4, (ib % 4) * E8
         return k, r0, (2 * k + c) * B + r0
 
     def opm_outer(ib, slot, fp):
         nat0 = opm_place(ib)[2]
         o = mm(at[rows_at(ib * W, W)], cp[fp * W:fp * W + W], NT)
-        for i in range(8):
+        for i in range(E8):
             nrow = ninv[pl.ds(nat0 + i, 1), :]
             for ff in range(2):
                 blk = o[B * i:B * i + B, N * ff:N * ff + N] * nrow
@@ -402,11 +413,11 @@
     def opm_bias(p, us):
         k, r = pair_place(p)
         b = mm(wtsb[...].astype(BF16), layer_norm(nw[us, :, 0:N].astype(F32)), NT)
-        bs[rows_at(((2 * k + c) * B + r) * 8, T16)] = side_by_side(b).astype(BF16).astype(F32)
+        bs[rows_at(((2 * k + c) * B + r) * E8, T16)] = side_by_side(b).astype(BF16).astype(F32)
 
     def opm_two(t, carry):
-        for e in range(8):
-            p = 8 * t + e
+        for e in range(E8):
+            p = E8 * t + e
             slot = e // 4
             opm_bias(jnp.maximum(p - 2, 0), e % 2)
             opm_update(jnp.maximum(p - 1, 0), 1 - e % 2)
@@ -435,10 +446,10 @@
         cpy.wait_recv()
     mres = mrs[...]
     for h in range(4):
-        bts[h] = jnp.transpose(bs[pl.ds(h, N, stride=8), :]) * LOG2E + mres
+        bts[h] = jnp.transpose(bs[pl.ds(h, N, stride=E8), :]) * LOG2E + mres
 
     def zx_copy(ob):
-        rows = rows_at(ob * 8, 8)
+        rows = rows_at(ob * E8, E8)
         return remote(zs.at[rows], zx.at[c, rows], zx_s.at[ob], zx_r.at[ob], 1)
 
     def ts_x(p):
@@ -447,7 +458,7 @@
     def ts_post(p, slot):
         b = mm(wteb[...].astype(BF16), layer_norm(nw[slot, :, 0:N].astype(F32)), NT)
         nat = (2 * (p // T16) + c) * B + 2 * (p % T16)
-        be[rows_at(nat * 8, T16)] = side_by_side(b).astype(BF16).astype(F32)
+        be[rows_at(nat * E8, T16)] = side_by_side(b).astype(BF16).astype(F32)
 
     def ts_emit(p, slot, new):
         nw[slot, :, 0:N] = new.astype(BF16)
@@ -467,7 +478,7 @@
             zx_copy(ob - 1).start()
         return carry
     ts.begin()
-    lax.fori_loop(0, 8, ts_four, 0)
+    lax.fori_loop(0, E8, ts_four, 0)
     ts.end(31)
     zx_copy(7).start()
     be_copies = tri_bias_copies(be, be_s, be_r)
@@ -476,12 +487,12 @@
     for cpy in be_copies:
         cpy.wait_recv()
     for h in range(4):
-        bte[h] = be[pl.ds(h, N, stride=8), :] * LOG2E + mres
+        bte[h] = be[pl.ds(h, N, stride=E8), :] * LOG2E + mres
 
     def zx_wait(ob, carry):
         zx_copy(ob).wait_recv()
         return carry
-    lax.fori_loop(0, 8, zx_wait, 0)
+    lax.fori_loop(0, E8, zx_wait, 0)
 
     def zo_copies(ci, q, hf):
         out = []
@@ -535,7 +546,7 @@
     def drain8(j, carry):
         zx_copy(j).wait_send()
         return carry
-    lax.fori_loop(0, 8, drain8, 0)
+    lax.fori_loop(0, E8, drain8, 0)
     for t in range(4):
         xb_copy(t).wait_send()
         for rel in range(2):
@@ -550,6 +561,22 @@
             cpy.wait()
         return carry
     lax.fori_loop(0, 4, drain4, 0)
+
+
+def finish(m_ref, z_ref, m_out, z_out, m_buf, z_buf, in_sem, out_sem):
+    steps = []
+    for n in range(E8):
+        for src, buf, dst, k in ((m_ref, m_buf, m_out, 0), (z_ref, z_buf, z_out, 1)):
+            at = (n // 4, pl.ds(n % 4 * E8, E8))
+            steps.append((pltpu.make_async_copy(src.at[at], buf.at[at], in_sem.at[k, n]),
+                          pltpu.make_async_copy(buf.at[at], dst.at[at], out_sem.at[k, n])))
+    for load, _ in steps:
+        load.start()
+    for load, store in steps:
+        load.wait()
+        store.start()
+    for _, store in steps:
+        store.wait()
 
 
 def weight_t(w):
@@ -574,20 +601,20 @@
         scratch = [V(shape, BF16) for shape in (
             (2,) + row_z, row_z, (2,) + row_m, (3, B, 2, B, W), (2, 64, 2, B, W), (K1, N), (K1, N))]
         scratch += [V(shape, F32) for shape in (
-            (K1, N), (2, 8) + sq) + ((N * COL_PITCH, N),) * 4]
+            (K1, N), (2, E8) + sq) + ((N * COL_PITCH, N),) * 4]
         scratch += [V((N, 2, B, W), BF16), V((2048, N), BF16), V((B * N, N), BF16), V((N * COL_PITCH, N), F32),
-                    V((B * N, N), BF16), V(sq, F32), V(sq, F32), V((N, K1), BF16), V((2, 8, K1, N), BF16)]
+                    V((B * N, N), BF16), V(sq, F32), V(sq, F32), V((N, K1), BF16), V((2, E8, K1, N), BF16)]
         scratch += [V(shape, F32) for shape in ((K1, N), (4,) + sq, (K1, N), (4,) + sq)]
-        scratch += [V((2, 64, 2, B, N), BF16), V((64, 2, B, N), BF16), V((N * TRI_PITCH, N), F32), V((N * TRI_PITCH, N), F32),
+        scratch += [V((2, 64, 2, B, N), BF16), V((64, 2, B, N), BF16),
                     V((N, 2, B, N), BF16)]
         scratch += [V((2, W, W), BF16)] * 2 + [V((4, W, W), BF16), V((4, W, W), F32), V((2, T16) + sq, F32),
-                    V((2, T16, N), F32), V((2, W, W), BF16), V((2, W, W), BF16), V((8, N), F32), V((8, N), F32)]
+                    V((2, T16, N), F32), V((2, W, W), BF16), V((2, W, W), BF16), V((2, W, W), BF16), V((E8, N), F32), V((E8, N), F32)]
         scratch += [V(sq, F32), V((2,) + sq, F32), V(sq, F32)] + [V((B,) + sq, F32)] * 2 + [V((2, N, W), F32)]
         S = pltpu.SemaphoreType.DMA
         scratch += [S(shape) for shape in (
-            (4,), (3,), (3,), (6,), (6,), (2, 4, 2), (2, 4, 2), (4,), (4,), (2, 3), (2, 3), (2,), (2,), (2,),
-            (2,), (2,), (2,), (2,), (8,), (8,), (4, 3), (4, 3), (4,))]
-        return pl.pallas_call(
+            (4,), (2,), (2,), (6,), (6,), (2, 4, 2), (2, 4, 2), (4,), (4,), (2, 3), (2, 3), (2,), (2,), (2,),
+            (2,), (2,), (2,), (2,), (E8,), (E8,), (4, 3), (4, 3), (4,))]
+        outs = pl.pallas_call(
             mega,
             out_shape=(jax.ShapeDtypeStruct(m.shape, BF16), jax.ShapeDtypeStruct(z.shape, BF16)),
             in_specs=[hbm, hbm] + [vm] * 15,
@@ -597,5 +624,13 @@
                                                  vmem_limit_bytes=62 << 20),
             name='evoformer_block',
         )(*args)
+        return pl.pallas_call(
+            finish,
+            out_shape=(jax.ShapeDtypeStruct(m.shape, BF16), jax.ShapeDtypeStruct(z.shape, BF16)),
+            in_specs=[hbm, hbm],
+            out_specs=(hbm, hbm),
+            scratch_shapes=[V(m.shape, BF16), V(z.shape, BF16), S((2, E8)), S((2, E8))],
+            name='finish',
+        )(*outs)
 
     return jax.shard_map(block, mesh=mesh, in_specs=in_specs, out_specs=(rows_spec, rows_spec), check_vma=False)

time: 156 us -> 158 us (1.013)
  Pallas kernels: 149 us -> 157 us
  local copies, waits for them, and re-layouts: 6.17 us -> 0 us
    unnamed x4 -> x0, local copies, waits for them, and re-layouts: 6.17 us -> none
    pallas_call x0 -> x1, Pallas kernels: none -> 5.53 us  [block(): pl.pallas_call(finish, out_shape=(jax.ShapeDtypeStruct(m.shape, BF16), ja...]
    pallas_call x1, Pallas kernels: 149 us -> 151 us  [block(): pl.pallas_call(mega, out_shape=(jax.ShapeDtypeStruct(m.shape, BF16), jax....]
where the time goes in v4:
time: 158 us
  Pallas kernels  157 us (99%)
    pallas_call x1, Pallas kernels, block(): pl.pallas_call(mega, out_shape=(jax.ShapeDtypeStruct(m.shape, BF16), jax....  151 us
    pallas_call x1, Pallas kernels, block(): pl.pallas_call(finish, out_shape=(jax.ShapeDtypeStruct(m.shape, BF16), ja...  5.53 us

profile of v4, /device:TPU:0, one launch (start us, length us, event | category | flops | bytes accessed | tf_op | source)
XLA Modules:
  0.0 157.5 jit_solution(11784775711270669948)
XLA Ops:
  0.6 151.2 %evoformer_block.1 = (bf16[2,32,128,256]{3,2,1,0:T(8,128)(2,1)}, bf16[2,32,128,128]{3,2,1,0:T(8,128)(2,1)}) custom-call(bf16[2,32,128,256]{3,2,1,0:T(8,128)(2,1)} %m_in.1, bf16[2,32,128,128]{3,2,1,0:T(8,128)(2,1)} %z_in.1, s32[2,128,128]{2,1,0:T(8,128)} %mask_ref.1, s32[2,128]{1,0:T(2,128)} %res_ref.1, bf16[8,128]{1,0:T(8,128)(2,1)} %bitcast.33, ...), custom_call_target="tpu_custom_call" | custom-call | tf_op jit(solution)/shard_map/evoformer_block/pallas_call | solution.py:617
  151.8 5.5 %finish.1 = (bf16[2,32,128,256]{3,2,1,0:T(8,128)(2,1)}, bf16[2,32,128,128]{3,2,1,0:T(8,128)(2,1)}) custom-call(bf16[2,32,128,256]{3,2,1,0:T(8,128)(2,1)} %get-tuple-element.4.m_ref, bf16[2,32,128,128]{3,2,1,0:T(8,128)(2,1)} %get-tuple-element.5.z_ref), custom_call_target="tpu_custom_call" | custom-call | tf_op jit(solution)/shard_map/finish/pallas_call | solution.py:627

commit v5 on v4

--- a/solution.py
+++ b/solution.py
@@ -185,9 +185,10 @@
     pl.semaphore_wait(barrier, 3)
 
     z_copies = []
-    for n, (first, size) in enumerate(((0, E8), (E8, 24))):
+    for n, (first, size) in enumerate(((0, 4), (4, E8), (12, 20))):
         rows = pl.ds(first, size)
         z_copies.append(remote(z_in.at[ox, rows], zr.at[x, rows], zi_s.at[n], zi_r.at[n], 2))
+    z_copies[0].start()
 
     row0 = pl.multiple_of(dev * W, W)
     own = pl.ds(row0, W)
@@ -210,7 +211,7 @@
     bias_rows(lambda r: zot[pl.ds(r, 2)], bbo)
     for cpy in b_copies[2:]:
         cpy.start()
-    z_copies[0].start()
+    z_copies[1].start()
 
     for wdst, wsrc in ((wtsb, w_tsb), (wteb, w_teb)):
         wdst[0:4] = wsrc[...].astype(F32)
@@ -291,7 +292,7 @@
             for tt in range(4):
                 for rel in range(2):
                     xa_copy(1, tt, rel).start()
-            z_copies[1].start()
+            z_copies[2].start()
 
         @pl.when(t > 4)
         def _():
@@ -381,16 +382,14 @@
         cp[rows_at(f * N, N)] = ctf[pl.ds(f, N, stride=COL_PITCH), :].astype(BF16)
         return carry
     lax.fori_loop(0, B, perm_c, 0)
-    for cpy in z_copies:
-        cpy.wait_recv()
 
     def opm_place(ib):
-        k, r0 = ib // 4, (ib % 4) * E8
+        k, r0 = jnp.where(ib < 4, x, ox), (ib % 4) * E8
         return k, r0, (2 * k + c) * B + r0
 
     def opm_outer(ib, slot, fp):
-        nat0 = opm_place(ib)[2]
-        o = mm(at[rows_at(ib * W, W)], cp[fp * W:fp * W + W], NT)
+        k, r0, nat0 = opm_place(ib)
+        o = mm(at[rows_at((k * B + r0) * B, W)], cp[fp * W:fp * W + W], NT)
         for i in range(E8):
             nrow = ninv[pl.ds(nat0 + i, 1), :]
             for ff in range(2):
@@ -398,7 +397,7 @@
                 rr[slot, i, fp * 64 + B * ff:fp * 64 + B * ff + B] = blk.astype(BF16)
 
     def pair_place(p):
-        return p // T16, 2 * (p % T16)
+        return jnp.where(p < T16, x, ox), 2 * (p % T16)
 
     def opm_product(slot, ip, us):
         ut[us] = mm(woot[...], jnp.concatenate([rr[slot, 2 * ip], rr[slot, 2 * ip + 1]], axis=1), NN)
@@ -416,6 +415,11 @@
         bs[rows_at(((2 * k + c) * B + r) * E8, T16)] = side_by_side(b).astype(BF16).astype(F32)
 
     def opm_two(t, carry):
+        @pl.when(t == 2)
+        def _():
+            for cpy in z_copies:
+                cpy.wait_recv()
+
         for e in range(E8):
             p = E8 * t + e
             slot = e // 4
@@ -612,7 +616,7 @@
         scratch += [V(sq, F32), V((2,) + sq, F32), V(sq, F32)] + [V((B,) + sq, F32)] * 2 + [V((2, N, W), F32)]
         S = pltpu.SemaphoreType.DMA
         scratch += [S(shape) for shape in (
-            (4,), (2,), (2,), (6,), (6,), (2, 4, 2), (2, 4, 2), (4,), (4,), (2, 3), (2, 3), (2,), (2,), (2,),
+            (4,), (3,), (3,), (6,), (6,), (2, 4, 2), (2, 4, 2), (4,), (4,), (2, 3), (2, 3), (2,), (2,), (2,),
             (2,), (2,), (2,), (2,), (E8,), (E8,), (4, 3), (4, 3), (4,))]
         outs = pl.pallas_call(
             mega,

time: 158 us -> 155 us (0.981)
  Pallas kernels: 157 us -> 154 us
    pallas_call x1, Pallas kernels: 151 us -> 149 us  [block(): pl.pallas_call(mega, out_shape=(jax.ShapeDtypeStruct(m.shape, BF16), jax....]
where the time goes in v5:
time: 155 us
  Pallas kernels  154 us (99%)
    pallas_call x1, Pallas kernels, block(): pl.pallas_call(mega, out_shape=(jax.ShapeDtypeStruct(m.shape, BF16), jax....  149 us
    pallas_call x1, Pallas kernels, block(): pl.pallas_call(finish, out_shape=(jax.ShapeDtypeStruct(m.shape, BF16), ja...  5.53 us

profile of v5, /device:TPU:0, one launch (start us, length us, event | category | flops | bytes accessed | tf_op | source)
XLA Modules:
  0.0 155.1 jit_solution(15371585220333008332)
XLA Ops:
  0.6 148.8 %evoformer_block.1 = (bf16[2,32,128,256]{3,2,1,0:T(8,128)(2,1)}, bf16[2,32,128,128]{3,2,1,0:T(8,128)(2,1)}) custom-call(bf16[2,32,128,256]{3,2,1,0:T(8,128)(2,1)} %m_in.1, bf16[2,32,128,128]{3,2,1,0:T(8,128)(2,1)} %z_in.1, s32[2,128,128]{2,1,0:T(8,128)} %mask_ref.1, s32[2,128]{1,0:T(2,128)} %res_ref.1, bf16[8,128]{1,0:T(8,128)(2,1)} %bitcast.33, ...), custom_call_target="tpu_custom_call" | custom-call | tf_op jit(solution)/shard_map/evoformer_block/pallas_call | solution.py:621
  149.5 5.5 %finish.1 = (bf16[2,32,128,256]{3,2,1,0:T(8,128)(2,1)}, bf16[2,32,128,128]{3,2,1,0:T(8,128)(2,1)}) custom-call(bf16[2,32,128,256]{3,2,1,0:T(8,128)(2,1)} %get-tuple-element.4.m_ref, bf16[2,32,128,128]{3,2,1,0:T(8,128)(2,1)} %get-tuple-element.5.z_ref), custom_call_target="tpu_custom_call" | custom-call | tf_op jit(solution)/shard_map/finish/pallas_call | solution.py:631
